TPU v7x, 32 devices: a whole 2x2x4 slice. The times are simulated.
32 devices in a mesh: seq: 8 (over z, x), fsdp: 4 (over y, core).
Axes of the slice: x: 2, y: 2, z: 4, core: 2. Of those that a mesh axis runs over, the one named last changes fastest.
Arguments:
- tokens: bfloat16 [4, 2048, 2048], P('fsdp', 'seq'), may hold values from -6 to 6
- routes: int32 [4, 2048, 8], P('fsdp', 'seq'), may hold values from 0 to 31, all different within a row; in each aligned block of 256 rows (0 to 255, 256 to 511, ..., all dimensions but the last counted through in order) at most 96 rows name the same one
- route_weights: float32 [4, 2048, 8], P('fsdp', 'seq'), may hold values from 0.05 to 0.5
- cotangent: bfloat16 [4, 2048, 2048], P('fsdp', 'seq'), may hold values from -6 to 6
- attn_gain: bfloat16 [2048], P('fsdp'), may hold values from 0.099609375 to 1.8984375
- query_gain: bfloat16 [2048], P('fsdp'), may hold values from 0.099609375 to 1.8984375
- key_gain: bfloat16 [2048], P('fsdp'), may hold values from 0.099609375 to 1.8984375
- ffn_gain: bfloat16 [2048], P('fsdp'), may hold values from 0.099609375 to 1.8984375
- w_query: bfloat16 [2048, 2048], P('fsdp'), may hold values from -0.125 to 0.125
- w_key: bfloat16 [2048, 2048], P('fsdp'), may hold values from -0.125 to 0.125
- w_value: bfloat16 [2048, 2048], P('fsdp'), may hold values from -0.125 to 0.125
- w_out: bfloat16 [2048, 2048], P('fsdp'), may hold values from -2 to 2
- w_gate: bfloat16 [2048, 32, 1024], P('fsdp', 'seq'), may hold values from -0.125 to 0.125
- w_up: bfloat16 [2048, 32, 1024], P('fsdp', 'seq'), may hold values from -0.125 to 0.125
- w_down: bfloat16 [2048, 32, 1024], P('fsdp', 'seq'), may hold values from -0.5 to 0.5
Outputs:
- block_out: bfloat16 [4, 2048, 2048], P('fsdp', 'seq')
- tokens_grad: float32 [4, 2048, 2048], P('fsdp', 'seq')
- attn_gain_grad: float32 [2048], P(('seq', 'fsdp'))
- query_gain_grad: float32 [2048], P(('seq', 'fsdp'))
- key_gain_grad: float32 [2048], P(('seq', 'fsdp'))
- ffn_gain_grad: float32 [2048], P(('seq', 'fsdp'))
- w_query_grad: float32 [2048, 2048], P(('seq', 'fsdp'))
- w_key_grad: float32 [2048, 2048], P(('seq', 'fsdp'))
- w_value_grad: float32 [2048, 2048], P(('seq', 'fsdp'))
- w_out_grad: float32 [2048, 2048], P(('seq', 'fsdp'))
- w_gate_grad: float32 [2048, 32, 1024], P('fsdp', 'seq')
- w_up_grad: float32 [2048, 32, 1024], P('fsdp', 'seq')
- w_down_grad: float32 [2048, 32, 1024], P('fsdp', 'seq')
Inputs may be any that keep to these rules, and one draw needn't show every extreme that they name: `routes`: the 8 experts of a token differ. Among the 256 tokens of one device (aligned blocks in sequence order) no expert is named more than 96 times, and in every draw some expert is named exactly 96 times there.
All inputs are finite; a program needn't handle non-finite values.
Results may differ from a plain program's by a relative error of at most 0.017.
Values may be sent and summed in bfloat16 or wider, within the bound.
A program may use at most 448 MiB of HBM per device.

v0:
```python
import jax
import jax.numpy as jnp
from jax import lax
from jax.sharding import PartitionSpec as P

H = 16


epsilon = 1e-05


def inverse_norm(values):
    return lax.rsqrt(jnp.mean(values * values, axis=-1, keepdims=True) + epsilon)


def norm_backward(values, factor, gain, upstream):
    normal = values * factor
    weighted = upstream * gain
    gain_term = jnp.sum(upstream * normal, axis=0)
    back = factor * (weighted - normal * jnp.mean(weighted * normal, axis=-1, keepdims=True))
    return (back, gain_term)


def rope_tables(positions, head_dim):
    half = head_dim // 2
    frequency = jnp.power(10000.0, -2.0 * jnp.arange(half, dtype=jnp.float32) / head_dim)
    angle = positions.astype(jnp.float32)[:, None] * frequency[None, :]
    return (jnp.cos(angle)[:, None, :], jnp.sin(angle)[:, None, :])


def rotate(values, cosine, sine):
    half = values.shape[-1] // 2
    first = values[..., :half]
    second = values[..., half:]
    return jnp.concatenate(
        [first * cosine - second * sine, second * cosine + first * sine], axis=-1
    )


def unrotate(grads, cosine, sine):
    half = grads.shape[-1] // 2
    first = grads[..., :half]
    second = grads[..., half:]
    return jnp.concatenate(
        [first * cosine + second * sine, second * cosine - first * sine], axis=-1
    )


def route_tables(flat_routes, experts, capacity, picks):
    count = flat_routes.shape[0]
    one_hot = (flat_routes[:, None] == jnp.arange(experts, dtype=jnp.int32)[None, :]).astype(
        jnp.int32
    )
    running = jnp.cumsum(one_hot, axis=0) - 1
    rank = jnp.sum(one_hot * running, axis=1)
    slots = flat_routes * capacity + rank
    owner = (
        jnp.zeros((experts * capacity,), jnp.int32)
        .at[slots]
        .set(jnp.arange(count, dtype=jnp.int32) // picks)
    )
    filled = jnp.zeros((experts * capacity,), jnp.float32).at[slots].set(1.0)
    return (slots, owner, filled)


def block_scores(start, query_rows, keys, scale):
    scores = (
        jnp.einsum("qhd,khd->hqk", query_rows, keys, preferred_element_type=jnp.float32) * scale
    )
    query_pos = start + jnp.arange(query_rows.shape[0], dtype=jnp.int32)
    key_pos = jnp.arange(keys.shape[0], dtype=jnp.int32)
    causal = query_pos[:, None] >= key_pos[None, :]
    return jnp.where(causal[None], scores, -1e30)


def local(
    tokens,
    routes,
    route_weights,
    cotangent,
    attn_gain,
    query_gain,
    key_gain,
    ffn_gain,
    w_query,
    w_key,
    w_value,
    w_out,
    w_gate,
    w_up,
    w_down,
):
    seq_devices = lax.axis_size("seq")
    width = tokens.shape[-1]
    inputs = tokens.reshape(-1, width).astype(jnp.float32)
    local_tokens = inputs.shape[0]
    picks = routes.shape[-1]
    flat_routes = routes.reshape(-1)
    mixing = route_weights.reshape(local_tokens, picks)
    local_experts = w_gate.shape[1]
    experts = local_experts * seq_devices
    capacity = 3 * local_tokens * picks // (2 * experts)
    head_dim = width // H
    local_heads = H // seq_devices
    seq_length = local_tokens * seq_devices
    block = min(512, seq_length)
    block_count = seq_length // block
    scale = head_dim ** (-0.5)
    fetched = (
        lax.all_gather(w_query, "fsdp", axis=0, tiled=True),
        lax.all_gather(w_key, "fsdp", axis=0, tiled=True),
        lax.all_gather(w_value, "fsdp", axis=0, tiled=True),
        lax.all_gather(w_out, "fsdp", axis=0, tiled=True),
        lax.all_gather(attn_gain, "fsdp", axis=0, tiled=True),
        lax.all_gather(query_gain, "fsdp", axis=0, tiled=True),
        lax.all_gather(key_gain, "fsdp", axis=0, tiled=True),
        lax.all_gather(ffn_gain, "fsdp", axis=0, tiled=True),
        lax.all_gather(w_gate, "fsdp", axis=0, tiled=True),
        lax.all_gather(w_up, "fsdp", axis=0, tiled=True),
        lax.all_gather(w_down, "fsdp", axis=0, tiled=True),
    )
    (
        full_query,
        full_key,
        full_value,
        full_out,
        gain_attn,
        gain_query,
        gain_key,
        gain_ffn,
        full_gate,
        full_up,
        full_down,
    ) = fetched
    gain_attn = gain_attn.astype(jnp.float32)
    gain_query = gain_query.astype(jnp.float32)
    gain_key = gain_key.astype(jnp.float32)
    gain_ffn = gain_ffn.astype(jnp.float32)
    positions = lax.axis_index("seq") * local_tokens + jnp.arange(local_tokens, dtype=jnp.int32)
    cosine, sine = rope_tables(positions, head_dim)
    norm_one = inverse_norm(inputs)
    normed = (inputs * norm_one * gain_attn).astype(jnp.bfloat16)
    query_proj = jnp.dot(normed, full_query, preferred_element_type=jnp.float32)
    key_proj = jnp.dot(normed, full_key, preferred_element_type=jnp.float32)
    value_proj = jnp.dot(normed, full_value, preferred_element_type=jnp.float32)
    query_factor = inverse_norm(query_proj)
    key_factor = inverse_norm(key_proj)
    query_rot = rotate(
        (query_proj * query_factor * gain_query).reshape(local_tokens, H, head_dim), cosine, sine
    ).astype(jnp.bfloat16)
    key_rot = rotate(
        (key_proj * key_factor * gain_key).reshape(local_tokens, H, head_dim), cosine, sine
    ).astype(jnp.bfloat16)
    value_send = value_proj.reshape(local_tokens, H, head_dim).astype(jnp.bfloat16)
    query_heads, key_heads, value_heads = (
        lax.all_to_all(query_rot, "seq", split_axis=1, concat_axis=0, tiled=True),
        lax.all_to_all(key_rot, "seq", split_axis=1, concat_axis=0, tiled=True),
        lax.all_to_all(value_send, "seq", split_axis=1, concat_axis=0, tiled=True),
    )

    def forward_block(index):
        start = index * block
        query_rows = lax.dynamic_slice_in_dim(query_heads, start, block, 0)
        scores = block_scores(start, query_rows, key_heads, scale)
        peak = jnp.max(scores, axis=-1, keepdims=True)
        total = jnp.log(jnp.sum(jnp.exp(scores - peak), axis=-1, keepdims=True)) + peak
        probs = jnp.exp(scores - total).astype(jnp.bfloat16)
        result = jnp.einsum("hqk,khd->qhd", probs, value_heads, preferred_element_type=jnp.float32)
        return (result.astype(jnp.bfloat16), total[..., 0])

    block_ids = jnp.arange(block_count, dtype=jnp.int32)
    heads_out, log_totals = lax.map(forward_block, block_ids)
    heads_out = heads_out.reshape(seq_length, local_heads, head_dim)
    context = lax.all_to_all(heads_out, "seq", split_axis=0, concat_axis=1, tiled=True).reshape(
        local_tokens, width
    )
    mid = inputs + jnp.dot(context, full_out, preferred_element_type=jnp.float32)
    norm_two = inverse_norm(mid)
    ffn_in = (mid * norm_two * gain_ffn).astype(jnp.bfloat16)
    slots, owner, filled = route_tables(flat_routes, experts, capacity, picks)
    send_rows = jnp.where(filled[:, None] > 0, ffn_in[owner], jnp.zeros((), jnp.bfloat16)).reshape(
        experts, capacity, width
    )
    received = lax.all_to_all(send_rows, "seq", split_axis=0, concat_axis=0, tiled=True).reshape(
        seq_devices, local_experts, capacity, width
    )
    gate = jnp.einsum("secd,def->secf", received, full_gate, preferred_element_type=jnp.float32)
    up_part = jnp.einsum("secd,def->secf", received, full_up, preferred_element_type=jnp.float32)
    sigmoid_gate = jax.nn.sigmoid(gate)
    activated = gate * sigmoid_gate
    hidden = (activated * up_part).astype(jnp.bfloat16)
    expert_out = jnp.einsum(
        "secf,def->secd", hidden, full_down, preferred_element_type=jnp.float32
    ).astype(jnp.bfloat16)
    returned = lax.all_to_all(
        expert_out.reshape(experts, capacity, width), "seq", split_axis=0, concat_axis=0, tiled=True
    ).reshape(experts * capacity, width)
    picked = returned[slots].astype(jnp.float32).reshape(local_tokens, picks, width)
    block_out = (mid + jnp.sum(picked * mixing[:, :, None], axis=1)).astype(jnp.bfloat16)
    refetched = (
        lax.all_gather(w_query, "fsdp", axis=0, tiled=True),
        lax.all_gather(w_key, "fsdp", axis=0, tiled=True),
        lax.all_gather(w_value, "fsdp", axis=0, tiled=True),
        lax.all_gather(w_out, "fsdp", axis=0, tiled=True),
        lax.all_gather(w_gate, "fsdp", axis=0, tiled=True),
        lax.all_gather(w_up, "fsdp", axis=0, tiled=True),
        lax.all_gather(w_down, "fsdp", axis=0, tiled=True),
    )
    back_query, back_key, back_value, back_out, back_gate, back_up, back_down = refetched
    out_grad = cotangent.reshape(local_tokens, width).astype(jnp.float32)
    slot_weight = jnp.zeros((experts * capacity,), jnp.float32).at[slots].set(mixing.reshape(-1))
    down_send = (
        (out_grad[owner] * slot_weight[:, None])
        .astype(jnp.bfloat16)
        .reshape(experts, capacity, width)
    )
    down_received = lax.all_to_all(
        down_send, "seq", split_axis=0, concat_axis=0, tiled=True
    ).reshape(seq_devices, local_experts, capacity, width)
    hidden_grad = jnp.einsum(
        "secd,def->secf", down_received, back_down, preferred_element_type=jnp.float32
    )
    slope = sigmoid_gate * (1.0 + gate * (1.0 - sigmoid_gate))
    gate_grad = (hidden_grad * up_part * slope).astype(jnp.bfloat16)
    up_grad = (hidden_grad * activated).astype(jnp.bfloat16)
    rows_grad = (
        jnp.einsum("secf,def->secd", gate_grad, back_gate, preferred_element_type=jnp.float32)
        + jnp.einsum("secf,def->secd", up_grad, back_up, preferred_element_type=jnp.float32)
    ).astype(jnp.bfloat16)
    gate_term = jnp.einsum(
        "secd,secf->def", received, gate_grad, preferred_element_type=jnp.float32
    )
    up_term = jnp.einsum("secd,secf->def", received, up_grad, preferred_element_type=jnp.float32)
    down_term = jnp.einsum(
        "secd,secf->def", down_received, hidden, preferred_element_type=jnp.float32
    )
    gate_sum, up_sum, down_sum = (
        lax.psum_scatter(
            gate_term.astype(jnp.bfloat16), "fsdp", scatter_dimension=0, tiled=True
        ).astype(jnp.float32),
        lax.psum_scatter(
            up_term.astype(jnp.bfloat16), "fsdp", scatter_dimension=0, tiled=True
        ).astype(jnp.float32),
        lax.psum_scatter(
            down_term.astype(jnp.bfloat16), "fsdp", scatter_dimension=0, tiled=True
        ).astype(jnp.float32),
    )
    rows_back = lax.all_to_all(
        rows_grad.reshape(experts, capacity, width), "seq", split_axis=0, concat_axis=0, tiled=True
    ).reshape(experts * capacity, width)
    ffn_in_grad = jnp.sum(
        rows_back[slots].astype(jnp.float32).reshape(local_tokens, picks, width), axis=1
    )
    mid_back, ffn_gain_term = norm_backward(mid, norm_two, gain_ffn, ffn_in_grad)
    mid_grad = out_grad + mid_back
    branch_grad = mid_grad.astype(jnp.bfloat16)
    out_term = jnp.einsum("td,te->de", context, branch_grad, preferred_element_type=jnp.float32)
    context_grad = jnp.einsum(
        "te,de->td", branch_grad, back_out, preferred_element_type=jnp.float32
    ).astype(jnp.bfloat16)
    heads_grad = lax.all_to_all(
        context_grad.reshape(local_tokens, H, head_dim),
        "seq",
        split_axis=1,
        concat_axis=0,
        tiled=True,
    )

    def backward_block(carry, index):
        key_acc, value_acc = carry
        start = index * block
        query_rows = lax.dynamic_slice_in_dim(query_heads, start, block, 0)
        grad_rows = lax.dynamic_slice_in_dim(heads_grad, start, block, 0)
        scores = block_scores(start, query_rows, key_heads, scale)
        probs = jnp.exp(scores - log_totals[index][..., None])
        probs_low = probs.astype(jnp.bfloat16)
        probs_grad = jnp.einsum(
            "qhd,khd->hqk", grad_rows, value_heads, preferred_element_type=jnp.float32
        )
        shifted = probs_grad - jnp.sum(probs * probs_grad, axis=-1, keepdims=True)
        score_grad = (probs * shifted * scale).astype(jnp.bfloat16)
        query_part = jnp.einsum(
            "hqk,khd->qhd", score_grad, key_heads, preferred_element_type=jnp.float32
        )
        key_acc = key_acc + jnp.einsum(
            "hqk,qhd->khd", score_grad, query_rows, preferred_element_type=jnp.float32
        )
        value_acc = value_acc + jnp.einsum(
            "hqk,qhd->khd", probs_low, grad_rows, preferred_element_type=jnp.float32
        )
        return ((key_acc, value_acc), query_part.astype(jnp.bfloat16))

    zero_heads = jnp.zeros((seq_length, local_heads, head_dim), jnp.float32)
    (key_acc, value_acc), query_parts = lax.scan(
        backward_block, (zero_heads, zero_heads), block_ids
    )
    query_parts = query_parts.reshape(seq_length, local_heads, head_dim)
    query_back, key_back, value_back = (
        lax.all_to_all(query_parts, "seq", split_axis=0, concat_axis=1, tiled=True),
        lax.all_to_all(
            key_acc.astype(jnp.bfloat16), "seq", split_axis=0, concat_axis=1, tiled=True
        ),
        lax.all_to_all(
            value_acc.astype(jnp.bfloat16), "seq", split_axis=0, concat_axis=1, tiled=True
        ),
    )
    query_normed_grad = unrotate(query_back.astype(jnp.float32), cosine, sine).reshape(
        local_tokens, width
    )
    key_normed_grad = unrotate(key_back.astype(jnp.float32), cosine, sine).reshape(
        local_tokens, width
    )
    query_proj_back, query_gain_term = norm_backward(
        query_proj, query_factor, gain_query, query_normed_grad
    )
    key_proj_back, key_gain_term = norm_backward(key_proj, key_factor, gain_key, key_normed_grad)
    query_proj_grad = query_proj_back.astype(jnp.bfloat16)
    key_proj_grad = key_proj_back.astype(jnp.bfloat16)
    value_proj_grad = value_back.reshape(local_tokens, width)
    query_term = jnp.einsum(
        "td,te->de", normed, query_proj_grad, preferred_element_type=jnp.float32
    )
    key_term = jnp.einsum("td,te->de", normed, key_proj_grad, preferred_element_type=jnp.float32)
    value_term = jnp.einsum(
        "td,te->de", normed, value_proj_grad, preferred_element_type=jnp.float32
    )
    normed_grad = (
        jnp.einsum("te,de->td", query_proj_grad, back_query, preferred_element_type=jnp.float32)
        + jnp.einsum("te,de->td", key_proj_grad, back_key, preferred_element_type=jnp.float32)
        + jnp.einsum("te,de->td", value_proj_grad, back_value, preferred_element_type=jnp.float32)
    )
    input_back, attn_gain_term = norm_backward(inputs, norm_one, gain_attn, normed_grad)
    tokens_grad = (mid_grad + input_back).reshape(tokens.shape)
    attn_sums = (
        lax.psum_scatter(query_term, ("seq", "fsdp"), scatter_dimension=0, tiled=True),
        lax.psum_scatter(key_term, ("seq", "fsdp"), scatter_dimension=0, tiled=True),
        lax.psum_scatter(value_term, ("seq", "fsdp"), scatter_dimension=0, tiled=True),
        lax.psum_scatter(out_term, ("seq", "fsdp"), scatter_dimension=0, tiled=True),
        lax.psum_scatter(attn_gain_term, ("seq", "fsdp"), scatter_dimension=0, tiled=True),
        lax.psum_scatter(query_gain_term, ("seq", "fsdp"), scatter_dimension=0, tiled=True),
        lax.psum_scatter(key_gain_term, ("seq", "fsdp"), scatter_dimension=0, tiled=True),
        lax.psum_scatter(ffn_gain_term, ("seq", "fsdp"), scatter_dimension=0, tiled=True),
    )
    (
        query_sum,
        key_sum,
        value_sum,
        out_sum,
        attn_gain_sum,
        query_gain_sum,
        key_gain_sum,
        ffn_gain_sum,
    ) = attn_sums
    return (
        block_out.reshape(tokens.shape),
        tokens_grad,
        attn_gain_sum,
        query_gain_sum,
        key_gain_sum,
        ffn_gain_sum,
        query_sum,
        key_sum,
        value_sum,
        out_sum,
        gate_sum,
        up_sum,
        down_sum,
    )


def solution(mesh):
    placed = (
        P("fsdp", "seq", None),
        P("fsdp", "seq", None),
        P("fsdp", "seq", None),
        P("fsdp", "seq", None),
        P("fsdp"),
        P("fsdp"),
        P("fsdp"),
        P("fsdp"),
        P("fsdp", None),
        P("fsdp", None),
        P("fsdp", None),
        P("fsdp", None),
        P("fsdp", "seq", None),
        P("fsdp", "seq", None),
        P("fsdp", "seq", None),
    )
    return jax.shard_map(
        local,
        mesh=mesh,
        in_specs=placed,
        out_specs=(
            P("fsdp", "seq", None),
            P("fsdp", "seq", None),
            P(("seq", "fsdp")),
            P(("seq", "fsdp")),
            P(("seq", "fsdp")),
            P(("seq", "fsdp")),
            P(("seq", "fsdp"), None),
            P(("seq", "fsdp"), None),
            P(("seq", "fsdp"), None),
            P(("seq", "fsdp"), None),
            P("fsdp", "seq", None),
            P("fsdp", "seq", None),
            P("fsdp", "seq", None),
        ),
        check_vma=False,
    )
```

profile of v0, /device:TPU:0, one launch (start us, length us, event | category | flops | bytes accessed | tf_op | source)
XLA Modules:
  0.0 2613.6 jit_solution(9601204726064067485)
XLA Ops:
  34.8 35.9 %all-gather.12.cloned.1.call-done = bf16[2048,2048]{1,0:T(8,128)(2,1)} async-done(((bf16[512,2048]{1,0:T(8,128)(2,1)}), bf16[2048,2048]{1,0:T(8,128)(2,1)}) %all-gather.12.cloned.1.call-update) | async-done | bytes 8388624 | tf_op jit(solution)/shard_map/all_gather | solution.py:110
  78.5 52.0 %all-gather.14.cloned.1.call-done = bf16[2048,2048]{1,0:T(8,128)(2,1)} async-done(((bf16[512,2048]{1,0:T(8,128)(2,1)}), bf16[2048,2048]{1,0:T(8,128)(2,1)}) %all-gather.14.cloned.1.call-update) | async-done | bytes 8388624 | tf_op jit(solution)/shard_map/all_gather | solution.py:111
  150.5 24.7 all-to-all-done.1
  179.5 10.9 all-gather.16.cloned.1.call-done
  190.4 12.4 copy.170
  202.8 6.3 convolution_convert_fusion.1
  222.9 18.1 all-to-all-done.2
  243.5 44.7 %while.27 = (s32[]{:T(128)}, bf16[4,512,2,128]{3,1,0,2:T(8,128)(2,1)}, f32[4,2,512]{2,1,0:T(2,128)}, s32[4]{0:T(128)S(1)}, bf16[2048,2,128]{2,0,1:T(8,128)(2,1)}...) while((s32[]{:T(128)}, ...), condition=%wide.region_6.7_spmd, body=%wide.region_3.6_spmd.sunk | while | flops 1097989632 | bytes 32019632 | solution.py:172
  303.2 15.9 reduce-window.6
  325.8 8.1 scatter_custom_fusion.1
  333.9 8.1 scatter_custom_fusion
  345.9 6.2 multiply_reduce_fusion.5
  353.7 15.9 gather_fusion
  369.6 11.5 broadcast_select_fusion
  394.1 18.1 gather_fusion.2
  412.5 8.1 scatter_custom_fusion.2
  420.6 13.4 multiply_convert_fusion.1
  434.0 226.6 %all-to-all-done.4 = bf16[32,96,2048]{2,1,0:T(8,128)(2,1)} async-done(((bf16[32,96,2048]{2,1,0:T(8,128)(2,1)}), bf16[32,96,2048]{2,1,0:T(8,128)(2,1)}, u32[]{:S(2)}, u32[]{:S(2)}) %all-to-all-start.4) | async-done | bytes 12582944 | tf_op jit(solution)/shard_map/all_to_all | solution.py:184
  666.3 22.6 fusion.91
  689.0 22.6 fusion.87
  711.5 227.1 %all-to-all-done.6 = bf16[32,96,2048]{2,1,0:T(8,128)(2,1)} async-done(((bf16[32,96,2048]{2,1,0:T(8,128)(2,1)}), bf16[32,96,2048]{2,1,0:T(8,128)(2,1)}, u32[]{:S(2)}, u32[]{:S(2)}) %all-to-all-start.6) | async-done | bytes 12582944 | tf_op jit(solution)/shard_map/all_to_all | solution.py:217
  938.7 29.9 %fusion.99 = (bf16[8,4,96,1024]{3,2,0,1:T(8,128)(2,1)}, bf16[8,4,96,1024]{3,2,0,1:T(8,128)(2,1)}, bf16[8,4,96,1024]{3,2,0,1:T(8,128)(2,1)}) fusion(f32[4,8,96,1024]{3,2,1,0:T(8,128)} %fusion.87, f32[4,8,96,1024]{3,2,1,0:T(8,128)} %fusion.91, bf16[2048,4,1024]{2,0,1:T(8,128)(2,1)} %all-gather.24.cloned.1.call-done, bf16[8,4,96,2048]{3,2,1,0:T(8,128)(2,1)} %bitcast.50), kind=kOutput, calls=%fused_computation.95 | convolution fusion | flops 12932087808 | bytes 73400320 | tf_op jit(solution)/shard_map/secd,def->secf/dot_general | solution.py:220
  968.6 21.3 fusion.109
  990.0 21.7 fusion.110
  1011.7 22.1 fusion.85
  1033.9 24.7 fusion.97
  1058.6 10.9 copy.190
  1074.9 21.0 fusion.111
  1096.0 18.0 convert_bitcast_fusion
  1119.5 227.8 %all-to-all-done.7 = bf16[32,96,2048]{2,1,0:T(8,128)(2,1)} async-done(((bf16[32,96,2048]{2,1,0:T(8,128)(2,1)}), bf16[32,96,2048]{2,1,0:T(8,128)(2,1)}, u32[]{:S(2)}, u32[]{:S(2)}) %all-to-all-start.7) | async-done | bytes 12582944 | tf_op jit(solution)/shard_map/all_to_all | solution.py:248
  1353.0 22.5 gather_fusion.3
  1375.5 248.9 %all-to-all-done.5 = bf16[32,96,2048]{2,1,0:T(8,128)(2,1)} async-done(((bf16[32,96,2048]{2,1,0:T(8,128)(2,1)}), bf16[32,96,2048]{2,1,0:T(8,128)(2,1)}, u32[]{:S(2)}, u32[]{:S(2)}) %all-to-all-start.5) | async-done | bytes 12582944 | tf_op jit(solution)/shard_map/all_to_all | solution.py:195
  1624.3 22.7 gather_fusion.1
  1647.1 11.4 convert_reduce_fusion
  1661.3 12.9 fusion.84
  1679.5 8.1 fusion.146
  1700.5 31.6 %all-to-all-done.8 = bf16[256,16,128]{2,0,1:T(8,128)(2,1)S(1)} async-done(((bf16[256,16,128]{2,0,1:T(8,128)(2,1)}), bf16[256,16,128]{2,0,1:T(8,128)(2,1)S(1)}, u32[]{:S(2)}, u32[]{:S(2)}) %all-to-all-start.8) | async-done | bytes 1048608 | tf_op jit(solution)/shard_map/all_to_all | solution.py:261
  1734.4 219.9 %while.28 = (s32[]{:T(128)}, f32[2048,2,128]{0,2,1:T(8,128)}, f32[2048,2,128]{0,2,1:T(8,128)}, bf16[4,512,2,128]{3,1,0,2:T(8,128)(2,1)}, s32[4]{0:T(128)S(1)}, /...) while((s32[]{:T(128)}, f32[2048,2,128]{0,2,1:T(8,128)}, ...), condition=%wide.region_19.20_spmd.clone, body=%wide.region_17.19_spmd.clone.sunk | while | flops 2742163968 | bytes 111444744 | solution.py:294
  1750.3 16.2 fusion.237
  1766.6 14.8 fusion.239
  1781.4 7.5 fusion.238
  1804.7 16.8 fusion.237
  1821.5 14.8 fusion.239
  1836.4 8.1 fusion.238
  1860.3 16.8 fusion.237
  1877.1 14.5 fusion.239
  1891.5 8.0 fusion.238
  1915.3 16.4 fusion.237
  1931.7 14.5 fusion.239
  1946.1 8.0 fusion.238
  1958.1 13.2 all-to-all-start.9
  1973.5 23.9 all-to-all-done.9
  2001.7 25.3 all-to-all-done.10
  2033.5 8.2 fusion.164
  2048.7 8.3 fusion.166
  2059.9 35.9 %all_to_all.140 = bf16[2048,2,128]{2,1,0:T(2,128)(2,1)S(1)} all-to-all(bf16[2048,2,128]{2,1,0:T(2,128)(2,1)S(1)} %copy.201), channel_id=1, replica_groups=mesh['seq'=8,'fsdp'=4] {'seq'}, dimensions={0} | all-to-all | bytes 2097152 | tf_op jit(solution)/shard_map/all_to_all | solution.py:303
  2096.5 8.3 fusion.144
  2122.3 51.4 %all-reduce.4 = (f32[2048]{0:T(1024)S(1)}, f32[2048]{0:T(1024)S(1)}, f32[2048]{0:T(1024)S(1)}, f32[2048]{0:T(1024)S(1)}) all-reduce(f32[2048]{0:T(1024)S(1)} %get-tuple-element.214, f32[2048]{0:T(1024)S(1)} %get-tuple-element.212, f32[2048]{0:T(1024)S(1)} %get-tuple-element.210, ...), channel_id=2, replica_groups=mesh['seq'=8,'fsdp'=4] {'seq','fsdp'}, use_global_device_ids=true, to_apply=%region_24.25.clone | all-reduce | flops 8192 | bytes 65536
  2179.5 8.6 copy.207
  2188.1 8.5 copy.208
  2196.6 8.6 copy.209
  2205.2 24.8 reduce-scatter.10.cloned.1.call-done
  2230.0 189.1 %reduce-scatter.8.cloned.1.call-done = f32[64,2048]{1,0:T(8,128)} async-done(((f32[2048,2048]{1,0:T(8,128)}), f32[64,2048]{1,0:T(8,128)}) %reduce-scatter.8.cloned.1.call-update) | async-done | bytes 524304 | tf_op jit(solution)/shard_map/reduce_scatter | solution.py:335
  2419.1 187.8 %reduce-scatter.12.cloned.1.call-done = f32[64,2048]{1,0:T(8,128)} async-done(((f32[2048,2048]{1,0:T(8,128)}), f32[64,2048]{1,0:T(8,128)}) %reduce-scatter.12.cloned.1.call-update) | async-done | bytes 524304 | tf_op jit(solution)/shard_map/reduce_scatter | solution.py:337
  (324 shorter events, 306.2 us)
Async XLA Ops:
  7.2 63.5 %all-gather.12.cloned.1.call-start = ((), (), s32[]{:S(2)}) async-start(), calls=%async_computation.19 | async-start | bytes 10485760 | tf_op jit(solution)/shard_map/all_gather | solution.py:110
  7.9 122.6 %all-gather.14.cloned.1.call-start = ((), (), s32[]{:S(2)}) async-start(), calls=%async_computation.20 | async-start | bytes 10485760 | tf_op jit(solution)/shard_map/all_gather | solution.py:111
  8.7 181.7 %all-gather.16.cloned.1.call-start = ((), (), s32[]{:S(2)}) async-start(), calls=%async_computation.21 | async-start | bytes 10485760 | tf_op jit(solution)/shard_map/all_gather | solution.py:112
  9.4 336.5 %all-gather.18.cloned.1.call-start = ((), (), s32[]{:S(2)}) async-start(), calls=%async_computation.22 | async-start | bytes 10485760 | tf_op jit(solution)/shard_map/all_gather | solution.py:113
  10.0 656.3 %all-gather.20.cloned.1.call-start = ((), (), s32[]{:S(2)}) async-start(), calls=%async_computation.23 | async-start | bytes 20971520 | tf_op jit(solution)/shard_map/all_gather | solution.py:118
  15.6 6.9 copy-start.55
  15.6 12.6 copy-start.56
  15.6 18.3 copy-start
  22.5 180.3 %copy-start.32 = (f32[4,1,512]{2,1,0:T(1,128)}, f32[4,1,512]{2,1,0:T(1,128)S(1)}, u32[]{:S(2)}) copy-start(f32[4,1,512]{2,1,0:T(1,128)S(1)} %convert_element_type.251) | copy-start | bytes 24580
  28.2 48.4 %copy-start.34 = (f32[4,1,512]{2,1,0:T(1,128)}, f32[4,1,512]{2,1,0:T(1,128)S(1)}, u32[]{:S(2)}) copy-start(f32[4,1,512]{2,1,0:T(1,128)S(1)} %convert_element_type.252) | copy-start | bytes 24580
  33.9 102.5 %copy-start.36 = (f32[4,1,512]{2,1,0:T(1,128)}, f32[4,1,512]{2,1,0:T(1,128)S(1)}, u32[]{:S(2)}) copy-start(f32[4,1,512]{2,1,0:T(1,128)S(1)} %convert_element_type.253) | copy-start | bytes 24580
  34.2 168.5 %copy-start.40 = (f32[256]{0:T(256)}, f32[256]{0:T(256)S(1)}, u32[]{:S(2)}) copy-start(f32[256]{0:T(256)S(1)} %add_rsqrt_fusion.3) | copy-start | bytes 3076
  34.8 104.4 %copy-start.28 = (f32[256,64]{1,0:T(8,128)}, f32[256,64]{1,0:T(8,128)S(1)}, u32[]{:S(2)}) copy-start(f32[256,64]{1,0:T(8,128)S(1)} %get-tuple-element.279) | copy-start | bytes 196612
  34.8 104.4 %copy-start.30 = (f32[256,64]{1,0:T(8,128)}, f32[256,64]{1,0:T(8,128)S(1)}, u32[]{:S(2)}) copy-start(f32[256,64]{1,0:T(8,128)S(1)} %get-tuple-element.280) | copy-start | bytes 196612
  143.5 31.8 %all-to-all-start.1 = ((bf16[256,16,128]{2,0,1:T(8,128)(2,1)}), bf16[256,16,128]{2,0,1:T(8,128)(2,1)}, u32[]{:S(2)}, u32[]{:S(2)}) async-start(bf16[256,16,128]{2,0,1:T(8,128)(2,1)} %pad_maximum_fusion.1), calls=%async_computation.1 | async-start | bytes 2097152 | tf_op jit(solution)/shard_map/all_to_all | solution.py:157
  175.3 33.9 %all-to-all-start = ((bf16[256,16,128]{2,0,1:T(8,128)(2,1)}), bf16[256,16,128]{2,0,1:T(8,128)(2,1)S(1)}, u32[]{:S(2)}, u32[]{:S(2)}) async-start(bf16[256,16,128]{2,0,1:T(8,128)(2,1)} %pad_maximum_fusion), calls=%async_computation | async-start | bytes 2097152 | tf_op jit(solution)/shard_map/all_to_all | solution.py:156
  209.1 31.9 %all-to-all-start.2 = ((bf16[256,16,128]{2,0,1:T(8,128)(2,1)}), bf16[256,16,128]{2,0,1:T(8,128)(2,1)}, u32[]{:S(2)}, u32[]{:S(2)}) async-start(bf16[256,16,128]{2,0,1:T(8,128)(2,1)} %convolution_convert_fusion.1), calls=%async_computation.2 | async-start | bytes 2097152 | tf_op jit(solution)/shard_map/all_to_all | solution.py:158
  214.8 474.2 %all-gather.22.cloned.1.call-start = ((), (), s32[]{:S(2)}) async-start(), calls=%async_computation.24 | async-start | bytes 20971520 | tf_op jit(solution)/shard_map/all_gather | solution.py:119
  288.2 56.2 %copy-start.2 = (bf16[2048,2,128]{2,0,1:T(8,128)(2,1)}, bf16[2048,2,128]{2,0,1:T(8,128)(2,1)S(1)}, u32[]{:S(2)}) copy-start(bf16[2048,2,128]{2,0,1:T(8,128)(2,1)S(1)} %get-tuple-element.510) | copy-start | bytes 3145732
  288.2 56.2 %copy-start.4 = (bf16[2048,2,128]{2,0,1:T(8,128)(2,1)}, bf16[2048,2,128]{2,0,1:T(8,128)(2,1)S(1)}, u32[]{:S(2)}) copy-start(bf16[2048,2,128]{2,0,1:T(8,128)(2,1)S(1)} %get-tuple-element.511) | copy-start | bytes 3145732
  288.2 8.3 copy-start.45
  288.2 8.7 copy-start.57
  292.3 49.8 %all-to-all-start.3 = ((bf16[2048,2,128]{2,1,0:T(2,128)(2,1)}), bf16[2048,2,128]{2,1,0:T(2,128)(2,1)}, u32[]{:S(2)}, u32[]{:S(2)}) async-start(bf16[2048,2,128]{2,1,0:T(2,128)(2,1)} %copy.173), calls=%async_computation.3 | async-start | bytes 2097152 | tf_op jit(solution)/shard_map/all_to_all | solution.py:174
  302.5 49.7 %copy-start.38 = (f32[4,1,512]{2,1,0:T(1,128)}, f32[4,1,512]{2,1,0:T(1,128)S(1)}, u32[]{:S(2)}) copy-start(f32[4,1,512]{2,1,0:T(1,128)S(1)} %convert_element_type.254) | copy-start | bytes 24580
  325.8 86.7 %copy-start.46 = (s32[2048,1]{0,1:T(1,128)}, s32[2048,1]{0,1:T(1,128)S(1)}, u32[]{:S(2)}) copy-start(s32[2048,1]{0,1:T(1,128)S(1)} %compare_select_fusion) | copy-start | bytes 24580
  345.9 6.2 copy-start.17
  352.2 17.5 copy-start.52
  381.1 279.5 %all-to-all-start.4 = ((bf16[32,96,2048]{2,1,0:T(8,128)(2,1)}), bf16[32,96,2048]{2,1,0:T(8,128)(2,1)}, u32[]{:S(2)}, u32[]{:S(2)}) async-start(bf16[32,96,2048]{2,1,0:T(8,128)(2,1)} %broadcast_select_fusion), calls=%async_computation.4 | async-start | bytes 25165824 | tf_op jit(solution)/shard_map/all_to_all | solution.py:184
  387.0 551.7 %all-gather.24.cloned.1.call-start = ((), (), s32[]{:S(2)}) async-start(), calls=%async_computation.25 | async-start | bytes 20971520 | tf_op jit(solution)/shard_map/all_gather | solution.py:120
  394.1 18.1 copy-start.43
  660.6 278.0 %all-to-all-start.6 = ((bf16[32,96,2048]{2,1,0:T(8,128)(2,1)}), bf16[32,96,2048]{2,1,0:T(8,128)(2,1)}, u32[]{:S(2)}, u32[]{:S(2)}) async-start(bf16[32,96,2048]{2,1,0:T(8,128)(2,1)} %multiply_convert_fusion.1), calls=%async_computation.6 | async-start | bytes 25165824 | tf_op jit(solution)/shard_map/all_to_all | solution.py:217
  666.0 1513.5 %reduce-scatter.16.cloned.1.call-start = ((), (), s32[]{:S(2)}) async-start(), calls=%async_computation.30 | async-start | bytes 20971520 | tf_op jit(solution)/shard_map/reduce_scatter | solution.py:238
  989.9 1198.2 %reduce-scatter.18.cloned.1.call-start = ((), (), s32[]{:S(2)}) async-start(), calls=%async_computation.31 | async-start | bytes 20971520 | tf_op jit(solution)/shard_map/reduce_scatter | solution.py:241
  1069.5 277.8 %all-to-all-start.7 = ((bf16[32,96,2048]{2,1,0:T(8,128)(2,1)}), bf16[32,96,2048]{2,1,0:T(8,128)(2,1)}, u32[]{:S(2)}, u32[]{:S(2)}) async-start(bf16[32,96,2048]{2,1,0:T(8,128)(2,1)} %bitcast.341), calls=%async_computation.7 | async-start | bytes 25165824 | tf_op jit(solution)/shard_map/all_to_all | solution.py:248
  1074.9 1121.7 %reduce-scatter.20.cloned.1.call-start = ((), (), s32[]{:S(2)}) async-start(), calls=%async_computation.32 | async-start | bytes 20971520 | tf_op jit(solution)/shard_map/reduce_scatter | solution.py:244
  1347.3 5.5 copy-start.44
  1347.3 5.7 copy-start.47
  1347.3 277.1 %all-to-all-start.5 = ((bf16[32,96,2048]{2,1,0:T(8,128)(2,1)}), bf16[32,96,2048]{2,1,0:T(8,128)(2,1)}, u32[]{:S(2)}, u32[]{:S(2)}) async-start(bf16[32,96,2048]{2,1,0:T(8,128)(2,1)} %bitcast.342), calls=%async_computation.5 | async-start | bytes 25165824 | tf_op jit(solution)/shard_map/all_to_all | solution.py:195
  1352.8 852.5 %reduce-scatter.14.cloned.1.call-start = ((), (), s32[]{:S(2)}) async-start(), calls=%async_computation.29 | async-start | bytes 17301504 | tf_op jit(solution)/shard_map/reduce_scatter | solution.py:338
  1647.0 11.5 copy-start.7
  1647.1 11.4 copy-start.39
  1647.1 11.4 copy-start.53
  1661.3 13.0 copy-start.20
  1674.2 5.3 copy-start.18
  1694.9 39.5 %copy-start.3 = (bf16[2048,2,128]{2,0,1:T(8,128)(2,1)S(1)}, bf16[2048,2,128]{2,0,1:T(8,128)(2,1)}, u32[]{:S(2)}) copy-start(bf16[2048,2,128]{2,0,1:T(8,128)(2,1)} %copy-done.2) | copy-start | bytes 3145732
  1694.9 39.5 %copy-start.5 = (bf16[2048,2,128]{2,0,1:T(8,128)(2,1)S(1)}, bf16[2048,2,128]{2,0,1:T(8,128)(2,1)}, u32[]{:S(2)}) copy-start(bf16[2048,2,128]{2,0,1:T(8,128)(2,1)} %copy-done.4) | copy-start | bytes 3145732
  1696.2 36.0 %all-to-all-start.8 = ((bf16[256,16,128]{2,0,1:T(8,128)(2,1)}), bf16[256,16,128]{2,0,1:T(8,128)(2,1)S(1)}, u32[]{:S(2)}, u32[]{:S(2)}) async-start(bf16[256,16,128]{2,0,1:T(8,128)(2,1)} %bitcast.363), calls=%async_computation.8 | async-start | bytes 2097152 | tf_op jit(solution)/shard_map/all_to_all | solution.py:261
  1954.3 16.9 copy-start.27
  1958.1 39.3 %all-to-all-start.9 = ((bf16[2048,2,128]{2,1,0:T(2,128)(2,1)}), bf16[2048,2,128]{2,1,0:T(2,128)(2,1)S(1)}, u32[]{:S(2)}, u32[]{:S(2)}) async-start(bf16[2048,2,128]{2,1,0:T(2,128)(2,1)} %copy.194), calls=%async_computation.9 | async-start | bytes 2097152 | tf_op jit(solution)/shard_map/all_to_all | solution.py:299
  1997.4 29.6 %all-to-all-start.10 = ((bf16[2048,2,128]{2,1,0:T(2,128)(2,1)}), bf16[2048,2,128]{2,1,0:T(2,128)(2,1)S(1)}, u32[]{:S(2)}, u32[]{:S(2)}) async-start(bf16[2048,2,128]{2,1,0:T(2,128)(2,1)} %copy.198), calls=%async_computation.10 | async-start | bytes 2097152 | tf_op jit(solution)/shard_map/all_to_all | solution.py:300
  2001.1 229.0 %reduce-scatter.10.cloned.1.call-start = ((), (), s32[]{:S(2)}) async-start(), calls=%async_computation.27 | async-start | bytes 17301504 | tf_op jit(solution)/shard_map/reduce_scatter | solution.py:336
  2001.5 25.8 copy-start.29
  2001.5 25.7 copy-start.31
  2041.8 377.4 %reduce-scatter.8.cloned.1.call-start = ((), (), s32[]{:S(2)}) async-start(), calls=%async_computation.26 | async-start | bytes 17301504 | tf_op jit(solution)/shard_map/reduce_scatter | solution.py:335
  2041.8 4.9 copy-start.15
  2041.8 4.9 copy-start.16
  2057.0 549.9 %reduce-scatter.12.cloned.1.call-start = ((), (), s32[]{:S(2)}) async-start(), calls=%async_computation.28 | async-start | bytes 17301504 | tf_op jit(solution)/shard_map/reduce_scatter | solution.py:337
  2096.5 8.3 copy-start.25
  2106.1 6.0 copy-start.22
  2106.1 12.1 slice-start
  2112.1 6.0 slice-start.1
  2112.1 6.0 copy-start.26
  2118.2 4.1 copy-start.42
  2118.2 57.8 %copy-start.10 = (f32[256,2048]{1,0:T(8,128)S(1)}, f32[256,2048]{1,0:T(8,128)}, u32[]{:S(2)}) copy-start(f32[256,2048]{1,0:T(8,128)} %copy-done.8) | copy-start | bytes 6291460
  (21 other events, 35.3 us)
Sparse Core Ops, SparseCore 0:
  9.5 61.0 all-gather.11
  72.2 58.2 all-gather.13
  132.1 58.2 all-gather.15
  191.8 58.2 all-gather.17
  252.1 105.9 all-gather.19
  360.0 105.8 all-gather.21
  468.1 105.8 all-gather.23
  990.0 123.5 reduce-scatter.15
  1116.2 124.8 reduce-scatter.17
  1243.5 124.8 reduce-scatter.19
  1687.7 189.9 reduce-scatter.13
  2041.9 188.1 reduce-scatter.9
  2232.9 186.1 reduce-scatter.7
  2421.9 185.0 reduce-scatter.11
where the time goes:
time: 2620 us; the launch traced here: 2610 us
  waiting for transfers between devices  1560 us (60%)
  matrix products  509 us (19%)
  local copies, waits for them, and re-layouts  230 us (9%)
  other arithmetic  114 us (4%)
  blocking collectives  110 us (4%)
  starting transfers between devices  63.6 us (2%)
    all_to_all x1, waiting for transfers between devices, local(): lax.all_to_all(expert_out.reshape(experts, capacity, width), 'seq', split...  249 us
    all_to_all x1, waiting for transfers between devices, local(): lax.all_to_all(rows_grad.reshape(experts, capacity, width), 'seq', split_...  228 us
    all_to_all x1, waiting for transfers between devices, local(): lax.all_to_all(down_send, 'seq', split_axis=0, concat_axis=0, tiled=True)  227 us
    all_to_all x1, waiting for transfers between devices, local(): lax.all_to_all(send_rows, 'seq', split_axis=0, concat_axis=0, tiled=True)  227 us
    reduce_scatter x1, waiting for transfers between devices, local(): lax.psum_scatter(query_term, ('seq', 'fsdp'), scatter_dimension=0, tiled=...  189 us
    reduce_scatter x1, waiting for transfers between devices, local(): lax.psum_scatter(value_term, ('seq', 'fsdp'), scatter_dimension=0, tiled=...  188 us
    dot_general x4, matrix products, backward_block(): jnp.einsum('hqk,qhd->khd', score_grad, query_rows, preferred_element_type...  66.2 us
    unnamed x138, local copies, waits for them, and re-layouts  58.8 us
  transfers between devices with their start and end apart: 25, of which 15 were waited for; matrix products, arithmetic and copies ran while one was open for 30% of the time, Pallas kernels for 0%

commit v1 on v0

v1 whole, which is shorter than its diff:
```python
import functools
import jax
import jax.numpy as jnp
from jax import lax
from jax.experimental import pallas as pl
from jax.experimental.pallas import tpu as pltpu
from jax.sharding import PartitionSpec as P

MESH = pl.DeviceIdType.MESH
ANY = pl.ANY


def greet(peers):
    barrier = pltpu.get_barrier_semaphore()
    for peer in peers:
        pl.semaphore_signal(barrier, inc=1, device_id={"seq": peer}, device_id_type=MESH)
    pl.semaphore_wait(barrier, len(peers))


def push(src, dst, send, recv, peer):
    return pltpu.make_async_remote_copy(
        src_ref=src, dst_ref=dst, send_sem=send, recv_sem=recv,
        device_id={"seq": peer}, device_id_type=MESH)


def gather_kernel(n, pieces, own, out, send_sem, recv_sem, copy_sem):
    pair = 2
    lines = n // pair
    me = lax.axis_index("seq")
    a, b = me // pair, me % pair
    column = [((a + k) % lines) * pair + b for k in range(1, lines)]
    back = [((a + lines - k) % lines) * pair + b for k in range(1, lines)]
    across = a * pair + (1 - b)
    greet(column + [across])
    rows = own.shape[0] // pieces
    local = pltpu.make_async_copy(own, out.at[me], copy_sem)
    local.start()

    def piece(p):
        return pl.ds(p * rows, rows)

    sends = []
    for p in range(pieces):
        for k in range(lines):
            peer = across if k == 0 else column[k - 1]
            copy = push(own.at[piece(p)], out.at[me, piece(p)], send_sem.at[k, p], recv_sem.at[k, p], peer)
            copy.start()
            sends.append(copy)
    relays = []
    for p in range(pieces):
        for k in range(1, lines):
            src = back[k - 1]
            push(own.at[piece(p)], out.at[src, piece(p)], send_sem.at[k, p], recv_sem.at[k, p], across).wait_recv()
            slot = lines + k - 1
            copy = push(out.at[src, piece(p)], out.at[src, piece(p)], send_sem.at[slot, p], recv_sem.at[slot, p], across)
            copy.start()
            relays.append(copy)
    for p in range(pieces):
        push(own.at[piece(p)], out.at[across, piece(p)], send_sem.at[0, p], recv_sem.at[0, p], across).wait_recv()
    for copy in relays:
        copy.wait_recv()
    for copy in sends + relays:
        copy.wait_send()
    local.wait()


def gather_rows(x, n, pieces=4, collective_id=0):
    slots = n // 2 + n // 2 - 1
    return pl.pallas_call(
        functools.partial(gather_kernel, n, pieces),
        out_shape=jax.ShapeDtypeStruct((n,) + x.shape, x.dtype),
        in_specs=[pl.BlockSpec(memory_space=pltpu.VMEM)],
        out_specs=pl.BlockSpec(memory_space=ANY),
        scratch_shapes=[
            pltpu.SemaphoreType.DMA((slots, pieces)),
            pltpu.SemaphoreType.DMA((slots, pieces)),
            pltpu.SemaphoreType.DMA,
        ],
        compiler_params=pltpu.CompilerParams(collective_id=collective_id, has_side_effects=True),
        name="gather_rows",
    )(x)


def reduce_kernel(n, pieces, part, out, mine, got, sums, landed, send_sem, recv_sem, load_sem):
    pair = 2
    lines = n // pair
    me = lax.axis_index("seq")
    a, b = me // pair, me % pair
    column = [((a + k) % lines) * pair + b for k in range(1, lines)]
    across = a * pair + (1 - b)
    greet(column + [across])
    rows = out.shape[0] // pieces
    order = list(range(1, lines)) + [0]

    def piece(p):
        return pl.ds(p * rows, rows)

    firsts, loads = {}, {}
    for k in order:
        line = (a + k) % lines
        for p in range(pieces):
            copy = push(part.at[line * pair + (1 - b), piece(p)], got.at[k, piece(p)],
                        send_sem.at[k, p], recv_sem.at[k, p], across)
            copy.start()
            firsts[k, p] = copy
            load = pltpu.make_async_copy(part.at[line * pair + b, piece(p)], mine.at[k, piece(p)], load_sem.at[k, p])
            load.start()
            loads[k, p] = load
    seconds = {}
    for k in order:
        for p in range(pieces):
            firsts[k, p].wait_recv()
            loads[k, p].wait()
            total = mine[k, piece(p)].astype(jnp.float32) + got[k, piece(p)].astype(jnp.float32)
            if k:
                sums[k - 1, piece(p)] = total.astype(jnp.bfloat16)
                slot = lines + k - 1
                copy = push(sums.at[k - 1, piece(p)], landed.at[k - 1, piece(p)],
                            send_sem.at[slot, p], recv_sem.at[slot, p], column[k - 1])
                copy.start()
                seconds[k, p] = copy
            else:
                for j in range(1, lines):
                    seconds[j, p].wait_recv()
                    total += landed[j - 1, piece(p)].astype(jnp.float32)
                out[piece(p), :] = total
    for copy in list(firsts.values()) + list(seconds.values()):
        copy.wait_send()


def reduce_rows(part, n, pieces=4, collective_id=1):
    _, rows, width = part.shape
    lines = n // 2
    slots = lines + lines - 1
    return pl.pallas_call(
        functools.partial(reduce_kernel, n, pieces),
        out_shape=jax.ShapeDtypeStruct((rows, width), jnp.float32),
        in_specs=[pl.BlockSpec(memory_space=ANY)],
        out_specs=pl.BlockSpec(memory_space=pltpu.VMEM),
        scratch_shapes=[
            pltpu.VMEM((lines, rows, width), jnp.bfloat16),
            pltpu.VMEM((lines, rows, width), jnp.bfloat16),
            pltpu.VMEM((lines - 1, rows, width), jnp.bfloat16),
            pltpu.VMEM((lines - 1, rows, width), jnp.bfloat16),
            pltpu.SemaphoreType.DMA((slots, pieces)),
            pltpu.SemaphoreType.DMA((slots, pieces)),
            pltpu.SemaphoreType.DMA((lines, pieces)),
        ],
        compiler_params=pltpu.CompilerParams(collective_id=collective_id, has_side_effects=True),
        name="reduce_rows",
    )(part)


def sum_kernel(n, own, sent, out, taken, landed, send_sem, recv_sem, copy_sem):
    me = lax.axis_index("seq")
    peers = [(me + k) % n for k in range(1, n)]
    greet(peers)
    local = pltpu.make_async_copy(sent.at[me], taken.at[me], copy_sem)
    local.start()
    copies, swaps = [], []
    for k in range(1, n):
        copy = push(own, landed.at[k - 1], send_sem.at[0, k - 1], recv_sem.at[0, k - 1], peers[k - 1])
        copy.start()
        copies.append(copy)
        swap = push(sent.at[peers[k - 1]], taken.at[me], send_sem.at[1, k - 1], recv_sem.at[1, k - 1], peers[k - 1])
        swap.start()
        swaps.append(swap)
    total = own[...]
    for k in range(1, n):
        copies[k - 1].wait_recv()
        total = total + landed[k - 1]
    out[...] = total
    for copy in copies:
        copy.wait_send()
    for swap in swaps:
        swap.wait()
    local.wait()


def sum_rows(x, sent, n, collective_id):
    return pl.pallas_call(
        functools.partial(sum_kernel, n),
        out_shape=(
            jax.ShapeDtypeStruct(x.shape, x.dtype),
            jax.ShapeDtypeStruct(sent.shape, sent.dtype),
        ),
        in_specs=[pl.BlockSpec(memory_space=pltpu.VMEM)] * 2,
        out_specs=[pl.BlockSpec(memory_space=pltpu.VMEM)] * 2,
        scratch_shapes=[
            pltpu.VMEM((n - 1,) + x.shape, x.dtype),
            pltpu.SemaphoreType.DMA((2, n - 1)),
            pltpu.SemaphoreType.DMA((2, n - 1)),
            pltpu.SemaphoreType.DMA,
        ],
        compiler_params=pltpu.CompilerParams(collective_id=collective_id, has_side_effects=True),
        name="sum_rows",
    )(x, sent)


H = 16
epsilon = 1e-05


def inverse_norm(values):
    return lax.rsqrt(jnp.mean(values * values, axis=-1, keepdims=True) + epsilon)


def norm_backward(values, factor, gain, upstream):
    normal = values * factor
    weighted = upstream * gain
    gain_term = jnp.sum(upstream * normal, axis=0)
    back = factor * (weighted - normal * jnp.mean(weighted * normal, axis=-1, keepdims=True))
    return (back, gain_term)


def rope_tables(positions, head_dim):
    half = head_dim // 2
    frequency = jnp.power(10000.0, -2.0 * jnp.arange(half, dtype=jnp.float32) / head_dim)
    angle = positions.astype(jnp.float32)[:, None] * frequency[None, :]
    return (jnp.cos(angle)[:, None, :], jnp.sin(angle)[:, None, :])


def rotate(values, cosine, sine):
    half = values.shape[-1] // 2
    first = values[..., :half]
    second = values[..., half:]
    return jnp.concatenate(
        [first * cosine - second * sine, second * cosine + first * sine], axis=-1
    )


def unrotate(grads, cosine, sine):
    half = grads.shape[-1] // 2
    first = grads[..., :half]
    second = grads[..., half:]
    return jnp.concatenate(
        [first * cosine + second * sine, second * cosine - first * sine], axis=-1
    )


def block_scores(start, query_rows, keys, scale):
    scores = (
        jnp.einsum("qhd,khd->hqk", query_rows, keys, preferred_element_type=jnp.float32) * scale
    )
    query_pos = start + jnp.arange(query_rows.shape[0], dtype=jnp.int32)
    key_pos = jnp.arange(keys.shape[0], dtype=jnp.int32)
    causal = query_pos[:, None] >= key_pos[None, :]
    return jnp.where(causal[None], scores, -1e30)


def gather_async(x, n):
    pair = 2
    lines = n // pair
    across = [(a * pair + b, a * pair + 1 - b) for a in range(lines) for b in range(pair)]
    column = [x]
    for k in range(1, lines):
        column.append(
            lax.ppermute(
                x, "seq", [(a * pair + b, (a + k) % lines * pair + b) for a in range(lines) for b in range(pair)]
            )
        )
    other = [lax.ppermute(c, "seq", across) for c in column]
    me = lax.axis_index("seq")
    a, b = me // pair, me % pair
    out = jnp.zeros((n,) + x.shape, x.dtype)
    for k in range(lines):
        line = (a + lines - k) % lines
        out = lax.dynamic_update_index_in_dim(out, column[k], line * pair + b, 0)
        out = lax.dynamic_update_index_in_dim(out, other[k], line * pair + 1 - b, 0)
    return out


def reduce_async(part, n):
    pair = 2
    lines = n // pair
    me = lax.axis_index("seq")
    a, b = me // pair, me % pair
    across = [(c * pair + d, c * pair + 1 - d) for c in range(lines) for d in range(pair)]
    halves = part.reshape(lines, pair, *part.shape[1:])
    give = lax.dynamic_index_in_dim(halves, 1 - b, 1, keepdims=False)
    keep = lax.dynamic_index_in_dim(halves, b, 1, keepdims=False)
    got = lax.ppermute(give, "seq", across)
    sums = (keep.astype(jnp.float32) + got.astype(jnp.float32)).astype(part.dtype)
    total = lax.dynamic_index_in_dim(sums, a, 0, keepdims=False).astype(jnp.float32)
    for k in range(1, lines):
        shift = [(c * pair + d, (c + k) % lines * pair + d) for c in range(lines) for d in range(pair)]
        piece = lax.dynamic_index_in_dim(sums, (a + k) % lines, 0, keepdims=False)
        total = total + lax.ppermute(piece, "seq", shift).astype(jnp.float32)
    return total


def local(
    tokens, routes, route_weights, cotangent, attn_gain, query_gain, key_gain, ffn_gain,
    w_query, w_key, w_value, w_out, w_gate, w_up, w_down,
):
    n = lax.axis_size("seq")
    groups = lax.axis_size("fsdp")
    me = lax.axis_index("seq")
    width = tokens.shape[-1]
    own_tokens = tokens.reshape(-1, width)
    rows = own_tokens.shape[0]
    length = rows * n
    picks = routes.shape[-1]
    shard = w_query.shape[0]
    local_experts = w_gate.shape[1]
    experts = local_experts * n
    hidden_width = w_gate.shape[2]
    capacity = 3 * rows * picks // (2 * experts)
    head_dim = width // H
    heads = H // n
    span = heads * head_dim
    scale = head_dim ** (-0.5)
    bf, f32 = jnp.bfloat16, jnp.float32

    cols = lambda w: lax.dynamic_slice_in_dim(w, me * span, span, 1)
    w_heads = jnp.concatenate([cols(w_query), cols(w_key), cols(w_value)], axis=1)
    w_heads = lax.all_gather(w_heads, "fsdp", axis=0, tiled=True)
    full_out = lax.all_gather(w_out, "fsdp", axis=0, tiled=True)
    gains = lax.all_gather(
        jnp.stack([attn_gain, query_gain, key_gain, ffn_gain]), "fsdp", axis=1, tiled=True
    ).astype(f32)
    gain_attn, gain_ffn = gains[0], gains[3]
    gain_query = lax.dynamic_slice_in_dim(gains[1], me * span, span, 0)
    gain_key = lax.dynamic_slice_in_dim(gains[2], me * span, span, 0)
    by_expert = lambda w: lax.all_gather(jnp.swapaxes(w, 0, 1), "fsdp", axis=1, tiled=True)
    full_gate, full_up, full_down = by_expert(w_gate), by_expert(w_up), by_expert(w_down)

    expert_ids = jnp.arange(experts, dtype=jnp.int32)
    named = routes.reshape(rows, picks)[None] == expert_ids[:, None, None]
    mixing = route_weights.reshape(rows, picks)[None]
    sent = jnp.sum(jnp.where(named, mixing, 0.0), axis=-1).reshape(n, local_experts, rows)

    inputs_all = gather_rows(own_tokens, n, 8, 0).reshape(length, width)
    cot_own, inputs_all = lax.optimization_barrier((cotangent.reshape(rows, width), inputs_all))
    cot_all = gather_async(cot_own, n)
    inputs_all = inputs_all.astype(f32)
    norm_all = inverse_norm(inputs_all)
    normed = (inputs_all * norm_all * gain_attn).astype(bf)
    proj = jnp.dot(normed, w_heads, preferred_element_type=f32)
    query_proj, key_proj, value_proj = proj[:, :span], proj[:, span : 2 * span], proj[:, 2 * span :]
    squares = jnp.stack([jnp.sum(query_proj**2, -1), jnp.sum(key_proj**2, -1)]).reshape(-1, 128)
    squares, weights = sum_rows(squares, sent, n, 1)
    factors = lax.rsqrt(squares.reshape(2, length, 1) / width + epsilon)
    query_factor, key_factor = factors[0], factors[1]
    cosine, sine = rope_tables(jnp.arange(length, dtype=jnp.int32), head_dim)
    split = lambda v: v.reshape(length, heads, head_dim)
    queries = rotate(split(query_proj * query_factor * gain_query), cosine, sine).astype(bf)
    keys = rotate(split(key_proj * key_factor * gain_key), cosine, sine).astype(bf)
    values = split(value_proj).astype(bf)

    block = min(512, length)
    block_ids = jnp.arange(length // block, dtype=jnp.int32)

    def forward_block(index):
        start = index * block
        query_rows = lax.dynamic_slice_in_dim(queries, start, block, 0)
        scores = block_scores(start, query_rows, keys, scale)
        peak = jnp.max(scores, axis=-1, keepdims=True)
        total = jnp.log(jnp.sum(jnp.exp(scores - peak), axis=-1, keepdims=True)) + peak
        probs = jnp.exp(scores - total).astype(bf)
        result = jnp.einsum("hqk,khd->qhd", probs, values, preferred_element_type=f32)
        return (result.astype(bf), total[..., 0])

    heads_out, log_totals = lax.map(forward_block, block_ids)
    heads_out = heads_out.reshape(length, heads, head_dim)
    context = lax.all_to_all(
        heads_out.reshape(length, span), "seq", split_axis=0, concat_axis=1, tiled=True
    )
    inputs = own_tokens.astype(f32)
    mid = inputs + jnp.dot(context, full_out, preferred_element_type=f32)
    norm_two = inverse_norm(mid)
    ffn_in = (mid * norm_two * gain_ffn).astype(bf)

    ffn_all = gather_rows(ffn_in, n, 8, 2)
    taken = weights > 0
    tri = (jnp.arange(rows)[:, None] <= jnp.arange(rows)[None, :]).astype(bf)
    rank = jnp.einsum("cet,tu->ceu", taken.astype(bf), tri, preferred_element_type=f32) - 1.0
    slot_ids = jnp.arange(capacity, dtype=f32)
    hit = (rank[:, :, None, :] == slot_ids[None, None, :, None]) & taken[:, :, None, :]
    place = hit.astype(bf)
    slot_weight = jnp.sum(jnp.where(hit, weights[:, :, None, :], 0.0), axis=-1)
    slot_weight = jnp.swapaxes(slot_weight, 0, 1)[..., None]
    place_rows = lambda v: jnp.einsum("cert,ctd->ecrd", place, v, preferred_element_type=f32)
    received = place_rows(ffn_all).astype(bf)
    gate = jnp.einsum("ecrd,edf->ecrf", received, full_gate, preferred_element_type=f32)
    up_part = jnp.einsum("ecrd,edf->ecrf", received, full_up, preferred_element_type=f32)
    sigmoid_gate = jax.nn.sigmoid(gate)
    activated = gate * sigmoid_gate
    hidden = (activated * up_part).astype(bf)
    expert_out = jnp.einsum("ecrf,edf->ecrd", hidden, full_down, preferred_element_type=f32)
    expert_out = (expert_out * slot_weight).astype(bf)
    unplace = lambda v: jnp.einsum("cert,ecrd->ctd", place, v, preferred_element_type=f32).astype(bf)
    ffn_out = reduce_async(unplace(expert_out), n)
    block_out = (mid + ffn_out).astype(bf)

    out_grad = cotangent.reshape(rows, width).astype(f32)
    down_received = (place_rows(cot_all) * slot_weight).astype(bf)
    hidden_grad = jnp.einsum("ecrd,edf->ecrf", down_received, full_down, preferred_element_type=f32)
    slope = sigmoid_gate * (1.0 + gate * (1.0 - sigmoid_gate))
    gate_grad = (hidden_grad * up_part * slope).astype(bf)
    up_grad = (hidden_grad * activated).astype(bf)
    rows_grad = (
        jnp.einsum("ecrf,edf->ecrd", gate_grad, full_gate, preferred_element_type=f32)
        + jnp.einsum("ecrf,edf->ecrd", up_grad, full_up, preferred_element_type=f32)
    ).astype(bf)
    term = lambda a, b: jnp.einsum("ecrd,ecrf->edf", a, b, preferred_element_type=f32).astype(bf)
    scatter = lambda v: jnp.swapaxes(
        lax.psum_scatter(v, "fsdp", scatter_dimension=1, tiled=True).astype(f32), 0, 1
    )
    rows_part, down_term, gate_term, up_term = lax.optimization_barrier(
        (
            unplace(rows_grad),
            term(down_received, hidden),
            term(received, gate_grad),
            term(received, up_grad),
        )
    )
    down_sum, gate_sum, up_sum = scatter(down_term), scatter(gate_term), scatter(up_term)
    ffn_in_grad = reduce_rows(rows_part, n, 8, 4)
    mid_back, ffn_gain_term = norm_backward(mid, norm_two, gain_ffn, ffn_in_grad)
    mid_grad = out_grad + mid_back
    branch_grad = mid_grad.astype(bf)

    branch_all = gather_rows(branch_grad, n, 8, 5).reshape(length, width)
    out_rows = lax.dynamic_slice_in_dim(full_out, me * span, span, 0)
    heads_grad = split(
        jnp.einsum("te,de->td", branch_all, out_rows, preferred_element_type=f32).astype(bf)
    )
    out_term = jnp.einsum(
        "td,te->de", heads_out.reshape(length, span), branch_all, preferred_element_type=f32
    )
    out_sum = lax.psum_scatter(out_term, "fsdp", scatter_dimension=0, tiled=True)

    def backward_block(carry, index):
        key_acc, value_acc = carry
        start = index * block
        query_rows = lax.dynamic_slice_in_dim(queries, start, block, 0)
        grad_rows = lax.dynamic_slice_in_dim(heads_grad, start, block, 0)
        scores = block_scores(start, query_rows, keys, scale)
        probs = jnp.exp(scores - log_totals[index][..., None])
        probs_low = probs.astype(bf)
        probs_grad = jnp.einsum("qhd,khd->hqk", grad_rows, values, preferred_element_type=f32)
        shifted = probs_grad - jnp.sum(probs * probs_grad, axis=-1, keepdims=True)
        score_grad = (probs * shifted * scale).astype(bf)
        query_part = jnp.einsum("hqk,khd->qhd", score_grad, keys, preferred_element_type=f32)
        key_acc = key_acc + jnp.einsum(
            "hqk,qhd->khd", score_grad, query_rows, preferred_element_type=f32
        )
        value_acc = value_acc + jnp.einsum(
            "hqk,qhd->khd", probs_low, grad_rows, preferred_element_type=f32
        )
        return ((key_acc, value_acc), query_part.astype(bf))

    zero_heads = jnp.zeros((length, heads, head_dim), f32)
    (key_acc, value_acc), query_parts = lax.scan(
        backward_block, (zero_heads, zero_heads), block_ids
    )
    query_back = query_parts.reshape(length, heads, head_dim).astype(f32)
    key_back = key_acc.astype(bf).astype(f32)
    value_grad = value_acc.astype(bf).reshape(length, span)
    query_up = unrotate(query_back, cosine, sine).reshape(length, span)
    key_up = unrotate(key_back, cosine, sine).reshape(length, span)
    query_normal, key_normal = query_proj * query_factor, key_proj * key_factor
    query_weighted, key_weighted = query_up * gain_query, key_up * gain_key
    means = jnp.stack(
        [jnp.sum(query_weighted * query_normal, -1), jnp.sum(key_weighted * key_normal, -1)]
    ).reshape(-1, 128)
    means, _ = sum_rows(means, jnp.zeros((n, 8, 128), f32), n, 6)
    means = means.reshape(2, length, 1) / width
    query_grad = (query_factor * (query_weighted - query_normal * means[0])).astype(bf)
    key_grad = (key_factor * (key_weighted - key_normal * means[1])).astype(bf)
    head_gains = jnp.stack(
        [jnp.sum(query_up * query_normal, axis=0), jnp.sum(key_up * key_normal, axis=0)]
    )
    proj_grad = jnp.concatenate([query_grad, key_grad, value_grad], axis=1)
    normed_part = jnp.einsum("te,de->td", proj_grad, w_heads, preferred_element_type=f32).astype(bf)
    normed_grad = reduce_rows(normed_part.reshape(n, rows, width), n, 8, 7)
    input_back, attn_gain_term = norm_backward(inputs, inverse_norm(inputs), gain_attn, normed_grad)
    tokens_grad = mid_grad + input_back
    head_term = jnp.einsum("td,te->de", normed, proj_grad, preferred_element_type=f32)
    part = width // (n * groups)
    head_term = lax.psum_scatter(
        head_term.astype(bf).reshape(n, groups, part, 3 * span).swapaxes(0, 1),
        "fsdp",
        scatter_dimension=0,
        tiled=True,
    ).reshape(n, part, 3, span)
    head_term = lax.all_to_all(head_term, "seq", split_axis=0, concat_axis=0, tiled=True)
    head_sums = [
        head_term[:, :, i].swapaxes(0, 1).reshape(part, width).astype(f32) for i in range(3)
    ]
    gain_terms = lax.psum_scatter(
        jnp.stack([attn_gain_term, ffn_gain_term]), ("seq", "fsdp"), scatter_dimension=1, tiled=True
    )
    head_gains = lax.psum_scatter(head_gains, "fsdp", scatter_dimension=1, tiled=True)
    return (
        block_out.reshape(tokens.shape),
        tokens_grad.reshape(tokens.shape),
        gain_terms[0],
        head_gains[0],
        head_gains[1],
        gain_terms[1],
        head_sums[0],
        head_sums[1],
        head_sums[2],
        out_sum,
        gate_sum,
        up_sum,
        down_sum,
    )


def solution(mesh):
    rows3 = P("fsdp", "seq", None)
    both = P(("seq", "fsdp"))
    both2 = P(("seq", "fsdp"), None)
    placed = (rows3,) * 4 + (P("fsdp"),) * 4 + (P("fsdp", None),) * 4 + (rows3,) * 3
    return jax.shard_map(
        local,
        mesh=mesh,
        in_specs=placed,
        out_specs=(rows3,) * 2 + (both,) * 4 + (both2,) * 4 + (rows3,) * 3,
        check_vma=False,
    )
```

time: 2620 us -> 1940 us (0.74)
  waiting for transfers between devices: 1560 us -> 533 us
  Pallas kernels: 0 us -> 568 us
  blocking collectives: 110 us -> 5.61 us
  local copies, waits for them, and re-layouts: 230 us -> 151 us
  starting transfers between devices: 63.6 us -> 31.5 us
    all_to_all x11 -> x2, waiting for transfers between devices: 1050 us -> 14.1 us  [the longest x1 12 us: local(): lax.all_to_all(heads_out.reshape(length, span), 'seq', split_axis=0, conc...]
    pallas_call x0 -> x7, Pallas kernels: none -> 568 us  [the longest x3 333 us: gather_rows(): pl.pallas_call(functools.partial(gather_kernel, n, pieces), out_shape=jax...]
    ppermute x0 -> x11, waiting for transfers between devices: none -> 261 us  [the longest x1 85.1 us: reduce_async(): got = lax.ppermute(give, 'seq', across)]
    reduce_scatter x7 -> x5, waiting for transfers between devices: 402 us -> 255 us  [the longest x3 240 us: local(): lax.psum_scatter(v, 'fsdp', scatter_dimension=1, tiled=True).astype(f32)]
    all_gather x7 -> x5, waiting for transfers between devices: 98.8 us -> 0.03 us  [the longest x1 0.02 us: local(): full_out = lax.all_gather(w_out, 'fsdp', axis=0, tiled=True)]
    gather x4 -> x0, local copies, waits for them, and re-layouts: 79.2 us -> none  [the longest x1 22.7 us: local(): returned[slots].astype(jnp.float32).reshape(local_tokens, picks, width)]
    all_to_all x11 -> x2, starting transfers between devices: 62.9 us -> 10.7 us  [the longest x1 5.53 us: local(): lax.all_to_all(head_term, 'seq', split_axis=0, concat_axis=0, tiled=True)]
    unnamed x1 -> x0, blocking collectives: 51.4 us -> none
  transfers between devices with their start and end apart: 25 -> 25, of which waited for: 15 -> 13; matrix products, arithmetic and copies ran while one was open for 30% -> 18% of each run, Pallas kernels for 0% -> 18%
where the time goes in v1:
time: 1940 us; the launch traced here: 1930 us
  Pallas kernels  568 us (29%)
  waiting for transfers between devices  533 us (27%)
  matrix products  504 us (26%)
  local copies, waits for them, and re-layouts  151 us (8%)
  other arithmetic  107 us (6%)
  starting transfers between devices  31.5 us (2%)
    pallas_call x3, Pallas kernels, gather_rows(): pl.pallas_call(functools.partial(gather_kernel, n, pieces), out_shape=jax...  333 us
    reduce_scatter x3, waiting for transfers between devices, local(): lax.psum_scatter(v, 'fsdp', scatter_dimension=1, tiled=True).astype(f32)  240 us
    pallas_call x2, Pallas kernels, reduce_rows(): pl.pallas_call(functools.partial(reduce_kernel, n, pieces), out_shape=jax...  191 us
    ppermute x1, waiting for transfers between devices, reduce_async(): got = lax.ppermute(give, 'seq', across)  85.1 us
    unnamed x138, local copies, waits for them, and re-layouts  84.2 us
    ppermute x3, waiting for transfers between devices, reduce_async(): total = total + lax.ppermute(piece, 'seq', shift).astype(jnp.float32)  75.5 us
    dot_general x4, matrix products, backward_block(): jnp.einsum('hqk,qhd->khd', score_grad, query_rows, preferred_element_type...  64.9 us
    ppermute x3, waiting for transfers between devices, gather_async(): lax.ppermute(x, 'seq', [(a * pair + b, (a + k) % lines * pair + b) for a...  63.7 us
  transfers between devices with their start and end apart: 25, of which 13 were waited for; matrix products, arithmetic and copies ran while one was open for 18% of the time, Pallas kernels for 18%

profile of v1, /device:TPU:0, one launch (start us, length us, event | category | flops | bytes accessed | tf_op | source)
XLA Modules:
  0.0 1929.4 jit_solution(8742204219141640937)
XLA Ops:
  17.2 5.6 copy.272
  22.9 112.6 %gather_rows.3 = bf16[8,256,2048]{2,1,0:T(8,128)(2,1)} custom-call(bf16[256,2048]{1,0:T(8,128)(2,1)} %bitcast.293), custom_call_target="tpu_custom_call" | custom-call | tf_op jit(solution)/shard_map/gather_rows/pallas_call | solution.py:69
  135.6 5.7 collective-permute-start.9
  142.4 5.5 copy.270
  148.2 5.6 all_gather.18
  164.0 44.3 %collective-permute-done.5 = bf16[256,2048]{1,0:T(8,128)(2,1)} collective-permute-done((bf16[256,2048]{1,0:T(8,128)(2,1)S(1)}, bf16[256,2048]{1,0:T(8,128)(2,1)}, u32[]{:S(2)}, u32[]{:S(2)}) %collective-permute-start.5) | collective-permute-done | bytes 1048608 | tf_op jit(solution)/shard_map/ppermute | solution.py:258
  211.0 19.4 %collective-permute-done.7 = bf16[256,2048]{1,0:T(8,128)(2,1)} collective-permute-done((bf16[256,2048]{1,0:T(8,128)(2,1)S(1)}, bf16[256,2048]{1,0:T(8,128)(2,1)}, u32[]{:S(2)}, u32[]{:S(2)}) %collective-permute-start.7) | collective-permute-done | bytes 1048608 | tf_op jit(solution)/shard_map/ppermute | solution.py:258
  239.8 36.6 %collective-permute-done.8 = bf16[256,2048]{1,0:T(8,128)(2,1)S(1)} collective-permute-done((bf16[256,2048]{1,0:T(8,128)(2,1)}, bf16[256,2048]{1,0:T(8,128)(2,1)S(1)}, u32[]{:S(2)}, u32[]{:S(2)}) %collective-permute-start.8) | collective-permute-done | bytes 1048608 | tf_op jit(solution)/shard_map/ppermute | solution.py:262
  280.8 11.2 fusion.127
  298.1 31.3 %sum_rows.2 = (f32[32,128]{1,0:T(8,128)}, f32[8,4,256]{2,1,0:T(4,128)}) custom-call(f32[32,128]{1,0:T(8,128)} %reshape.340.own, f32[8,4,256]{2,1,0:T(4,128)} %reshape.341.sent), custom_call_target="tpu_custom_call" | custom-call | tf_op jit(solution)/shard_map/sum_rows/pallas_call | solution.py:181
  359.0 46.5 %while.27 = (s32[]{:T(128)}, bf16[4,512,2,128]{3,2,1,0:T(2,128)(2,1)}, f32[4,2,512]{2,1,0:T(2,128)}, s32[4]{0:T(128)S(1)}, bf16[2048,2,128]{2,0,1:T(8,128)(2,1)}...) while((s32[]{:T(128)}, ...), condition=%wide.region_7.8_spmd, body=%wide.region_4.7_spmd.sunk | while | flops 1097989632 | bytes 32542912 | solution.py:364
  414.8 10.2 fusion.83
  425.0 12.0 all-to-all-done
  437.6 6.1 multiply_reduce_fusion.5
  445.5 107.1 %gather_rows.4 = bf16[8,256,2048]{2,1,0:T(8,128)(2,1)} custom-call(bf16[256,2048]{1,0:T(8,128)(2,1)} %multiply_convert_fusion.10.own), custom_call_target="tpu_custom_call" | custom-call | tf_op jit(solution)/shard_map/gather_rows/pallas_call | solution.py:69
  552.6 9.7 convert_bitcast_fusion
  562.3 22.6 %fusion.89 = f32[4,8,96,1024]{3,2,1,0:T(8,128)} fusion(bf16[4,2048,1024]{2,1,0:T(8,128)(2,1)} %all-gather.12.cloned.1.call-done, bf16[4,8,96,2048]{3,2,0,1:T(8,128)(2,1)} %convert_bitcast_fusion), kind=kOutput, calls=%fused_computation.78 | convolution fusion | flops 12884901888 | bytes 41943040 | tf_op jit(solution)/shard_map/ecrd,edf->ecrf/dot_general | solution.py:386
  584.9 22.8 %fusion.91 = f32[4,8,96,1024]{3,2,1,0:T(8,128)} fusion(bf16[4,2048,1024]{2,1,0:T(8,128)(2,1)} %all-gather.10.cloned.1.call-done, bf16[4,8,96,2048]{3,2,0,1:T(8,128)(2,1)} %convert_bitcast_fusion), kind=kOutput, calls=%fused_computation.80 | convolution fusion | flops 12884901888 | bytes 41943040 | tf_op jit(solution)/shard_map/ecrd,edf->ecrf/dot_general | solution.py:385
  607.7 30.4 %multiply_convert_fusion.3 = (bf16[4,8,96,1024]{3,2,1,0:T(8,128)(2,1)}, bf16[4,8,96,1024]{3,2,1,0:T(8,128)(2,1)}, bf16[4,8,96,1024]{3,2,1,0:T(8,128)(2,1)}) fusion(f32[4,8,96,1024]{3,2,1,0:T(8,128)} %fusion.91, f32[4,8,96,1024]{3,2,1,0:T(8,128)} %fusion.89, bf16[4,2048,1024]{2,1,0:T(8,128)(2,1)} %all-gather.14.cloned.1.call-done, ...), kind=kOutput, calls=%fused_computation.93 | convolution fusion | flops 12932087808 | bytes 73400320 | tf_op jit(solution)/shard_map/ecrd,edf->ecrf/dot_general | solution.py:398
  638.0 19.6 %bitcast_convert_fusion.2 = bf16[4,2048,1024]{2,1,0:T(8,128)(2,1)} fusion(bf16[4,8,96,2048]{3,2,0,1:T(8,128)(2,1)} %fusion.83, bf16[4,8,96,1024]{3,2,1,0:T(8,128)(2,1)} %get-tuple-element.363), kind=kOutput, calls=%fused_computation.66 | convolution fusion | flops 12893290496 | bytes 35651584 | tf_op jit(solution)/shard_map/ecrd,ecrf->edf/dot_general | solution.py:406
  657.6 20.0 %bitcast_convert_fusion.1 = bf16[4,2048,1024]{2,1,0:T(8,128)(2,1)} fusion(bf16[4,8,96,2048]{3,2,0,1:T(8,128)(2,1)} %convert_bitcast_fusion, bf16[4,8,96,1024]{3,2,1,0:T(8,128)(2,1)} %get-tuple-element.362), kind=kOutput, calls=%fused_computation.65 | convolution fusion | flops 12893290496 | bytes 35651584 | tf_op jit(solution)/shard_map/ecrd,ecrf->edf/dot_general | solution.py:406
  677.7 19.6 %bitcast_convert_fusion = bf16[4,2048,1024]{2,1,0:T(8,128)(2,1)} fusion(bf16[4,8,96,2048]{3,2,0,1:T(8,128)(2,1)} %convert_bitcast_fusion, bf16[4,8,96,1024]{3,2,1,0:T(8,128)(2,1)} %get-tuple-element.361), kind=kOutput, calls=%fused_computation.64 | convolution fusion | flops 12893290496 | bytes 35651584 | tf_op jit(solution)/shard_map/ecrd,ecrf->edf/dot_general | solution.py:406
  697.3 21.8 %fusion.95 = f32[4,8,96,2048]{3,2,0,1:T(8,128)} fusion(bf16[4,2048,1024]{2,1,0:T(8,128)(2,1)} %all-gather.12.cloned.1.call-done, bf16[4,8,96,1024]{3,2,1,0:T(8,128)(2,1)} %get-tuple-element.361), kind=kOutput, calls=%fused_computation.86 | convolution fusion | flops 12884901888 | bytes 48234496 | tf_op jit(solution)/shard_map/ecrf,edf->ecrd/dot_general | solution.py:404
  719.1 22.0 %fusion.97 = f32[4,8,96,2048]{3,2,0,1:T(8,128)} fusion(bf16[4,2048,1024]{2,1,0:T(8,128)(2,1)} %all-gather.10.cloned.1.call-done, bf16[4,8,96,1024]{3,2,1,0:T(8,128)(2,1)} %get-tuple-element.362), kind=kOutput, calls=%fused_computation.88 | convolution fusion | flops 12884901888 | bytes 48234496 | tf_op jit(solution)/shard_map/ecrf,edf->ecrd/dot_general | solution.py:403
  741.2 21.3 %bitcast_convert_fusion.3.part = bf16[8,256,2048]{2,1,0:T(8,128)(2,1)} fusion(f32[4,8,96,2048]{3,2,0,1:T(8,128)} %fusion.97, f32[4,8,96,2048]{3,2,0,1:T(8,128)} %fusion.95, f32[8,4,256]{2,1,0:T(4,128)S(1)} %copy-done.28, pred[8,4,256]{2,1,0:T(4,128)(4,1)S(1)} %copy-done.31), kind=kOutput, calls=%fused_computation.82 | convolution fusion | flops 3239575552 | bytes 58761216 | tf_op jit(solution)/shard_map/cert,ecrd->ctd/dot_general | solution.py:392
  762.5 96.7 %reduce_rows.2 = f32[256,2048]{1,0:T(8,128)} custom-call(bf16[8,256,2048]{2,1,0:T(8,128)(2,1)} %bitcast_convert_fusion.3.part), custom_call_target="tpu_custom_call" | custom-call | tf_op jit(solution)/shard_map/reduce_rows/pallas_call | solution.py:135
  865.7 113.1 %gather_rows.5 = bf16[8,256,2048]{2,1,0:T(8,128)(2,1)} custom-call(bf16[256,2048]{1,0:T(8,128)(2,1)} %fusion.163.own), custom_call_target="tpu_custom_call" | custom-call | tf_op jit(solution)/shard_map/gather_rows/pallas_call | solution.py:69
  978.8 7.1 convolution_convert_fusion.2
  985.9 190.8 %while.28 = (s32[]{:T(128)}, f32[2048,2,128]{0,2,1:T(8,128)}, f32[2048,2,128]{0,2,1:T(8,128)}, bf16[4,512,2,128]{3,1,0,2:T(8,128)(2,1)}, s32[4]{0:T(128)S(1)}, /...) while((s32[]{:T(128)}, f32[2048,2,128]{0,2,1:T(8,128)}, ...), condition=%wide.region_14.15_spmd.clone, body=%wide.region_12.14_spmd.clone.sunk | while | flops 2742163968 | bytes 149193040 | solution.py:455
  1001.9 14.4 fusion.220
  1016.4 15.8 fusion.218
  1039.0 5.8 fusion.219
  1049.5 14.4 fusion.220
  1064.0 16.4 fusion.218
  1087.2 5.8 fusion.219
  1097.7 14.4 fusion.220
  1112.2 16.4 fusion.218
  1135.4 5.8 fusion.219
  1145.9 14.4 fusion.220
  1160.3 16.4 fusion.218
  1204.6 12.5 sum_rows.3
  1221.7 11.9 convolution_convert_fusion.1
  1236.7 10.9 convolution_convert_fusion
  1247.6 94.7 %reduce_rows.3 = f32[256,2048]{1,0:T(8,128)} custom-call(bf16[8,256,2048]{2,1,0:T(8,128)(2,1)} %bitcast.303), custom_call_target="tpu_custom_call" | custom-call | tf_op jit(solution)/shard_map/reduce_rows/pallas_call | solution.py:135
  1348.2 22.3 %fusion.93 = f32[4,8,96,2048]{3,2,0,1:T(8,128)} fusion(bf16[4,2048,1024]{2,1,0:T(8,128)(2,1)} %all-gather.14.cloned.1.call-done, bf16[4,8,96,1024]{3,2,1,0:T(8,128)(2,1)} %get-tuple-element.363), kind=kOutput, calls=%fused_computation.84 | convolution fusion | flops 12884901888 | bytes 48234496 | tf_op jit(solution)/shard_map/ecrf,edf->ecrd/dot_general | solution.py:390
  1370.5 13.0 bitcast_convert_fusion.4
  1389.2 7.1 fusion.153
  1396.2 85.1 %collective-permute-done = bf16[4,256,2048]{2,1,0:T(8,128)(2,1)} collective-permute-done((bf16[4,256,2048]{2,1,0:T(8,128)(2,1)}, bf16[4,256,2048]{2,1,0:T(8,128)(2,1)}, u32[]{:S(2)}, u32[]{:S(2)}) %collective-permute-start) | collective-permute-done | bytes 4194336 | tf_op jit(solution)/shard_map/ppermute | solution.py:282
  1490.5 9.2 collective-permute-start.1
  1506.9 5.5 all-to-all-start.1
  1516.6 7.3 collective-permute-done.1
  1523.9 22.5 %collective-permute-done.3 = bf16[256,2048]{1,0:T(8,128)(2,1)} collective-permute-done((bf16[256,2048]{1,0:T(8,128)(2,1)}, bf16[256,2048]{1,0:T(8,128)(2,1)}, u32[]{:S(2)}, u32[]{:S(2)}) %collective-permute-start.3) | collective-permute-done | bytes 1048608 | tf_op jit(solution)/shard_map/ppermute | solution.py:288
  1546.4 45.7 %collective-permute-done.2 = bf16[256,2048]{1,0:T(8,128)(2,1)} collective-permute-done((bf16[256,2048]{1,0:T(8,128)(2,1)}, bf16[256,2048]{1,0:T(8,128)(2,1)}, u32[]{:S(2)}, u32[]{:S(2)}) %collective-permute-start.2) | collective-permute-done | bytes 1048608 | tf_op jit(solution)/shard_map/ppermute | solution.py:288
  1592.1 6.3 fusion.133
  1604.2 28.8 %reduce-scatter.20.cloned.1.call-done = bf16[4,512,1024]{2,1,0:T(8,128)(2,1)} async-done(((bf16[4,2048,1024]{2,1,0:T(8,128)(2,1)}), bf16[4,512,1024]{2,1,0:T(8,128)(2,1)}) %reduce-scatter.20.cloned.1.call-update) | async-done | bytes 4194320 | tf_op jit(solution)/shard_map/reduce_scatter | solution.py:408
  1633.0 6.6 convert_bitcast_fusion.1
  1639.7 15.1 copy.207
  1654.8 105.7 %reduce-scatter.18.cloned.1.call-done = bf16[4,512,1024]{2,1,0:T(8,128)(2,1)} async-done(((bf16[4,2048,1024]{2,1,0:T(8,128)(2,1)}), bf16[4,512,1024]{2,1,0:T(8,128)(2,1)}) %reduce-scatter.18.cloned.1.call-update) | async-done | bytes 4194320 | tf_op jit(solution)/shard_map/reduce_scatter | solution.py:408
  1760.5 6.6 convert_bitcast_fusion.2
  1767.2 15.2 copy.206
  1782.4 105.8 %reduce-scatter.16.cloned.1.call-done = bf16[4,512,1024]{2,1,0:T(8,128)(2,1)} async-done(((bf16[4,2048,1024]{2,1,0:T(8,128)(2,1)}), bf16[4,512,1024]{2,1,0:T(8,128)(2,1)}) %reduce-scatter.16.cloned.1.call-update) | async-done | bytes 4194320 | tf_op jit(solution)/shard_map/reduce_scatter | solution.py:408
  1888.2 6.7 convert_bitcast_fusion.3
  1894.9 12.7 copy.205
  1907.6 14.8 reduce-scatter.14.cloned.1.call-done
  (344 shorter events, 247.7 us)
Async XLA Ops:
  7.2 273.6 %all-gather.6.cloned.1.call-start = ((), (), s32[]{:S(2)}) async-start(), calls=%async_computation.9 | async-start | bytes 3932160 | tf_op jit(solution)/shard_map/all_gather | solution.py:317
  10.9 426.7 %all-gather.8.cloned.1.call-start = ((), (), s32[]{:S(2)}) async-start(), calls=%async_computation.10 | async-start | bytes 10485760 | tf_op jit(solution)/shard_map/all_gather | solution.py:318
  11.6 550.7 %all-gather.12.cloned.1.call-start = ((), (), s32[]{:S(2)}) async-start(), calls=%async_computation.12 | async-start | bytes 20971520 | tf_op jit(solution)/shard_map/all_gather | solution.py:325
  17.2 567.7 %all-gather.10.cloned.1.call-start = ((), (), s32[]{:S(2)}) async-start(), calls=%async_computation.11 | async-start | bytes 20971520 | tf_op jit(solution)/shard_map/all_gather | solution.py:325
  22.8 112.7 %copy-start.17 = (bf16[1,256,2048]{2,1,0:T(8,128)(2,1)S(1)}, bf16[1,256,2048]{2,1,0:T(8,128)(2,1)}, u32[]{:S(2)}) copy-start(bf16[1,256,2048]{2,1,0:T(8,128)(2,1)} %param.22) | copy-start | bytes 3145732
  22.8 584.8 %all-gather.14.cloned.1.call-start = ((), (), s32[]{:S(2)}) async-start(), calls=%async_computation.13 | async-start | bytes 20971520 | tf_op jit(solution)/shard_map/all_gather | solution.py:325
  135.6 12.5 copy-start.59
  135.6 12.5 copy-start.60
  135.6 12.5 copy-start.61
  135.6 12.5 copy-start.62
  135.6 73.9 %collective-permute-start.9 = (bf16[256,2048]{1,0:T(8,128)(2,1)S(1)}, bf16[256,2048]{1,0:T(8,128)(2,1)}, u32[]{:S(2)}, u32[]{:S(2)}) collective-permute-start(bf16[256,2048]{1,0:T(8,128)(2,1)S(1)} %bitcast.298), channel_id=1, source_target_pairs={{0,24},{4,28},{8,0},{12,4},{16,8},{20,12},{24,16},{28,20},{1,25},{... | collective-permute-start | bytes 3145736 | tf_op jit(solution)/shard_map/ppermute | solution.py:258
  141.3 89.1 %collective-permute-start.7 = (bf16[256,2048]{1,0:T(8,128)(2,1)S(1)}, bf16[256,2048]{1,0:T(8,128)(2,1)}, u32[]{:S(2)}, u32[]{:S(2)}) collective-permute-start(bf16[256,2048]{1,0:T(8,128)(2,1)S(1)} %bitcast.299), channel_id=1, source_target_pairs={{0,16},{4,20},{8,24},{12,28},{16,0},{20,4},{24,8},{28,12},{1,17},{... | collective-permute-start | bytes 3145736 | tf_op jit(solution)/shard_map/ppermute | solution.py:258
  141.3 67.0 %collective-permute-start.5 = (bf16[256,2048]{1,0:T(8,128)(2,1)S(1)}, bf16[256,2048]{1,0:T(8,128)(2,1)}, u32[]{:S(2)}, u32[]{:S(2)}) collective-permute-start(bf16[256,2048]{1,0:T(8,128)(2,1)S(1)} %bitcast.300), channel_id=1, source_target_pairs={{0,8},{4,12},{8,16},{12,20},{16,24},{20,28},{24,0},{28,4},{1,9},{5... | collective-permute-start | bytes 3145736 | tf_op jit(solution)/shard_map/ppermute | solution.py:258
  141.9 88.5 %collective-permute-start.4 = (bf16[256,2048]{1,0:T(8,128)(2,1)S(1)}, bf16[256,2048]{1,0:T(8,128)(2,1)}, u32[]{:S(2)}, u32[]{:S(2)}) collective-permute-start(bf16[256,2048]{1,0:T(8,128)(2,1)S(1)} %bitcast.301), channel_id=1, source_target_pairs={{0,4},{4,0},{8,12},{12,8},{16,20},{20,16},{24,28},{28,24},{1,5},{5... | collective-permute-start | bytes 3145736 | tf_op jit(solution)/shard_map/ppermute | solution.py:262
  158.9 121.9 %copy-start.55 = (f32[2048]{0:T(1024)}, f32[2048]{0:T(1024)S(1)}, u32[]{:S(2)}) copy-start(f32[2048]{0:T(1024)S(1)} %add_rsqrt_fusion.1) | copy-start | bytes 24580
  160.2 48.1 %copy-start.19 = (bf16[8,256,2048]{2,1,0:T(8,128)(2,1)}, bf16[8,256,2048]{2,1,0:T(8,128)(2,1)S(1)}, u32[]{:S(2)}) copy-start(bf16[8,256,2048]{2,1,0:T(8,128)(2,1)S(1)} %bitcast_dynamic-update-slice_fusion.8) | copy-start | bytes 25165828
  160.2 120.6 %copy-start.41 = (f32[1,2048]{1,0:T(1,128)}, f32[1,2048]{1,0:T(1,128)S(1)}, u32[]{:S(2)}) copy-start(f32[1,2048]{1,0:T(1,128)S(1)} %get-tuple-element.401) | copy-start | bytes 24580
  160.2 283.5 %copy-start.33 = (f32[1,2048]{1,0:T(1,128)}, f32[1,2048]{1,0:T(1,128)S(1)}, u32[]{:S(2)}) copy-start(f32[1,2048]{1,0:T(1,128)S(1)} %get-tuple-element.398) | copy-start | bytes 24580
  163.9 188.3 %copy-start.13 = (f32[2048,64]{1,0:T(8,128)}, f32[2048,64]{1,0:T(8,128)S(1)}, u32[]{:S(2)}) copy-start(f32[2048,64]{1,0:T(8,128)S(1)} %get-tuple-element.404) | copy-start | bytes 1572868
  163.9 188.3 %copy-start.15 = (f32[2048,64]{1,0:T(8,128)}, f32[2048,64]{1,0:T(8,128)S(1)}, u32[]{:S(2)}) copy-start(f32[2048,64]{1,0:T(8,128)S(1)} %get-tuple-element.405) | copy-start | bytes 1572868
  208.3 26.8 %collective-permute-start.6 = (bf16[256,2048]{1,0:T(8,128)(2,1)}, bf16[256,2048]{1,0:T(8,128)(2,1)}, u32[]{:S(2)}, u32[]{:S(2)}) collective-permute-start(bf16[256,2048]{1,0:T(8,128)(2,1)} %collective-permute-done.5), channel_id=1, source_target_pairs={{0,4},{4,0},{8,12},{12,8},{16,20},{20,16},{24,28},{28,24},{1,5},{5... | collective-permute-start | bytes 3145736 | tf_op jit(solution)/shard_map/ppermute | solution.py:262
  208.8 121.4 %copy-start.49 = (f32[1,256]{1,0:T(1,128)}, f32[1,256]{1,0:T(1,128)S(1)}, u32[]{:S(2)}) copy-start(f32[1,256]{1,0:T(1,128)S(1)} %get-tuple-element.408) | copy-start | bytes 3076
  208.8 121.4 %copy-start.51 = (f32[1,256]{1,0:T(1,128)}, f32[1,256]{1,0:T(1,128)S(1)}, u32[]{:S(2)}) copy-start(f32[1,256]{1,0:T(1,128)S(1)} %get-tuple-element.409) | copy-start | bytes 3076
  209.5 70.3 %collective-permute-start.10 = (bf16[256,2048]{1,0:T(8,128)(2,1)}, bf16[256,2048]{1,0:T(8,128)(2,1)S(1)}, u32[]{:S(2)}, u32[]{:S(2)}) collective-permute-start(bf16[256,2048]{1,0:T(8,128)(2,1)} %collective-permute-done.9), channel_id=1, source_target_pairs={{0,4},{4,0},{8,12},{12,8},{16,20},{20,16},{24,28},{28,24},{1,5},{5... | collective-permute-start | bytes 3145736 | tf_op jit(solution)/shard_map/ppermute | solution.py:262
  230.4 46.0 %collective-permute-start.8 = (bf16[256,2048]{1,0:T(8,128)(2,1)}, bf16[256,2048]{1,0:T(8,128)(2,1)S(1)}, u32[]{:S(2)}, u32[]{:S(2)}) collective-permute-start(bf16[256,2048]{1,0:T(8,128)(2,1)} %collective-permute-done.7), channel_id=1, source_target_pairs={{0,4},{4,0},{8,12},{12,8},{16,20},{20,16},{24,28},{28,24},{1,5},{5... | collective-permute-start | bytes 3145736 | tf_op jit(solution)/shard_map/ppermute | solution.py:262
  359.0 54.8 %copy-start.36 = (f32[8,4,256]{2,1,0:T(4,128)S(1)}, f32[8,4,256]{2,1,0:T(4,128)}, u32[]{:S(2)}) copy-start(f32[8,4,256]{2,1,0:T(4,128)} %get-tuple-element.117) | copy-start | bytes 98308
  405.5 19.5 %copy-start.7 = (bf16[2048,2,128]{2,0,1:T(8,128)(2,1)}, bf16[2048,2,128]{2,0,1:T(8,128)(2,1)S(1)}, u32[]{:S(2)}) copy-start(bf16[2048,2,128]{2,0,1:T(8,128)(2,1)S(1)} %get-tuple-element.614) | copy-start | bytes 3145732
  405.5 19.5 %copy-start.9 = (bf16[2048,2,128]{2,0,1:T(8,128)(2,1)}, bf16[2048,2,128]{2,0,1:T(8,128)(2,1)S(1)}, u32[]{:S(2)}) copy-start(bf16[2048,2,128]{2,0,1:T(8,128)(2,1)S(1)} %get-tuple-element.615) | copy-start | bytes 3145732
  408.6 28.5 %all-to-all-start = ((bf16[8,256,256]{2,1,0:T(8,128)(2,1)}), bf16[8,256,256]{2,1,0:T(8,128)(2,1)S(1)}, u32[]{:S(2)}, u32[]{:S(2)}) async-start(bf16[8,256,256]{2,1,0:T(8,128)(2,1)} %all_to_all.17), calls=%async_computation | async-start | bytes 2097152 | tf_op jit(solution)/shard_map/all_to_all | solution.py:366
  413.7 1087.5 %reduce-scatter.12.cloned.1.call-start = ((), (), s32[]{:S(2)}) async-start(), calls=%async_computation.14 | async-start | bytes 3932160 | tf_op jit(solution)/shard_map/reduce_scatter | solution.py:482
  413.8 138.8 %copy-start.30 = (pred[8,4,256]{2,1,0:T(4,128)(4,1)}, pred[8,4,256]{2,1,0:T(4,128)(4,1)S(1)}, u32[]{:S(2)}) copy-start(pred[8,4,256]{2,1,0:T(4,128)(4,1)S(1)} %broadcast_compare_fusion) | copy-start | bytes 24580
  414.0 138.6 %copy-start.27 = (f32[8,4,256]{2,1,0:T(4,128)}, f32[8,4,256]{2,1,0:T(4,128)S(1)}, u32[]{:S(2)}) copy-start(f32[8,4,256]{2,1,0:T(4,128)S(1)} %copy.179) | copy-start | bytes 98308
  443.7 109.0 %copy-start.3 = (f32[256,2048]{1,0:T(8,128)}, f32[256,2048]{1,0:T(8,128)S(1)}, u32[]{:S(2)}) copy-start(f32[256,2048]{1,0:T(8,128)S(1)} %get-tuple-element.407) | copy-start | bytes 6291460
  719.1 22.0 %copy-start.28 = (f32[8,4,256]{2,1,0:T(4,128)S(1)}, f32[8,4,256]{2,1,0:T(4,128)}, u32[]{:S(2)}) copy-start(f32[8,4,256]{2,1,0:T(4,128)} %copy-done.27) | copy-start | bytes 98308
  719.1 22.0 %copy-start.31 = (pred[8,4,256]{2,1,0:T(4,128)(4,1)S(1)}, pred[8,4,256]{2,1,0:T(4,128)(4,1)}, u32[]{:S(2)}) copy-start(pred[8,4,256]{2,1,0:T(4,128)(4,1)} %copy-done.30) | copy-start | bytes 24580
  762.4 96.7 %copy-start.4 = (f32[256,2048]{1,0:T(8,128)S(1)}, f32[256,2048]{1,0:T(8,128)}, u32[]{:S(2)}) copy-start(f32[256,2048]{1,0:T(8,128)} %copy-done.3) | copy-start | bytes 6291460
  762.4 96.7 %copy-start.34 = (f32[1,2048]{1,0:T(1,128)S(1)}, f32[1,2048]{1,0:T(1,128)}, u32[]{:S(2)}) copy-start(f32[1,2048]{1,0:T(1,128)} %copy-done.33) | copy-start | bytes 24580
  762.4 96.7 %copy-start.47 = (f32[256]{0:T(256)S(1)}, f32[256]{0:T(256)}, u32[]{:S(2)}) copy-start(f32[256]{0:T(256)} %copy-done.46) | copy-start | bytes 3076
  762.5 100.1 %copy-start.18 = (bf16[1,256,2048]{2,1,0:T(8,128)(2,1)S(1)}, bf16[1,256,2048]{2,1,0:T(8,128)(2,1)}, u32[]{:S(2)}) copy-start(bf16[1,256,2048]{2,1,0:T(8,128)(2,1)} %param.22) | copy-start | bytes 3145732
  1203.3 18.4 copy-start.22
  1203.3 18.4 copy-start.42
  1203.3 18.4 copy-start.56
  1221.6 11.9 copy-start.24
  1221.6 11.9 copy-start.26
  1235.5 276.9 %reduce-scatter.24.cloned.1.call-start = ((), (), s32[]{:S(2)}) async-start(), calls=%async_computation.20 | async-start | bytes 163840
  1247.6 97.0 %copy-start.45 = (f32[2048]{0:T(1024)S(1)}, f32[2048]{0:T(1024)}, u32[]{:S(2)}) copy-start(f32[2048]{0:T(1024)} %get-tuple-element.319) | copy-start | bytes 24580
  1342.3 172.2 %reduce-scatter.22.cloned.1.call-start = ((), (), s32[]{:S(2)}) async-start(), calls=%async_computation.19 | async-start | bytes 1081344
  1346.0 287.0 %reduce-scatter.20.cloned.1.call-start = ((), (), s32[]{:S(2)}) async-start(), calls=%async_computation.18 | async-start | bytes 20971520 | tf_op jit(solution)/shard_map/reduce_scatter | solution.py:408
  1346.8 413.8 %reduce-scatter.18.cloned.1.call-start = ((), (), s32[]{:S(2)}) async-start(), calls=%async_computation.17 | async-start | bytes 20971520 | tf_op jit(solution)/shard_map/reduce_scatter | solution.py:408
  1347.4 540.8 %reduce-scatter.16.cloned.1.call-start = ((), (), s32[]{:S(2)}) async-start(), calls=%async_computation.16 | async-start | bytes 20971520 | tf_op jit(solution)/shard_map/reduce_scatter | solution.py:408
  1348.1 574.2 %reduce-scatter.14.cloned.1.call-start = ((), (), s32[]{:S(2)}) async-start(), calls=%async_computation.15 | async-start | bytes 2621440 | tf_op jit(solution)/shard_map/reduce_scatter | solution.py:432
  1348.1 22.3 %copy-start.29 = (f32[8,4,256]{2,1,0:T(4,128)S(1)}, f32[8,4,256]{2,1,0:T(4,128)}, u32[]{:S(2)}) copy-start(f32[8,4,256]{2,1,0:T(4,128)} %copy-done.27) | copy-start | bytes 98308
  1348.2 22.3 %copy-start.32 = (pred[8,4,256]{2,1,0:T(4,128)(4,1)S(1)}, pred[8,4,256]{2,1,0:T(4,128)(4,1)}, u32[]{:S(2)}) copy-start(pred[8,4,256]{2,1,0:T(4,128)(4,1)} %copy-done.30) | copy-start | bytes 24580
  1348.2 22.3 %copy-start.44 = (f32[8,4,96]{2,1,0:T(4,128)S(1)}, f32[8,4,96]{2,1,0:T(4,128)}, u32[]{:S(2)}) copy-start(f32[8,4,96]{2,1,0:T(4,128)} %copy-done.43) | copy-start | bytes 36868
  1388.4 93.0 %collective-permute-start = (bf16[4,256,2048]{2,1,0:T(8,128)(2,1)}, bf16[4,256,2048]{2,1,0:T(8,128)(2,1)}, u32[]{:S(2)}, u32[]{:S(2)}) collective-permute-start(bf16[4,256,2048]{2,1,0:T(8,128)(2,1)} %dynamic-slice_bitcast_fusion.1), channel_id=1, source_target_pairs={{0,4},{4,0},{8,12},{12,8},{16,20},{20,16},{24,28},{28,24},{1,5},{5... | collective-permute-start | bytes 12582920 | tf_op jit(solution)/shard_map/ppermute | solution.py:282
  1488.8 103.3 %copy-start.5 = (f32[256,2048]{1,0:T(8,128)S(1)}, f32[256,2048]{1,0:T(8,128)}, u32[]{:S(2)}) copy-start(f32[256,2048]{1,0:T(8,128)} %copy-done.3) | copy-start | bytes 6291460
  1488.8 103.3 %copy-start.35 = (f32[1,2048]{1,0:T(1,128)S(1)}, f32[1,2048]{1,0:T(1,128)}, u32[]{:S(2)}) copy-start(f32[1,2048]{1,0:T(1,128)} %copy-done.33) | copy-start | bytes 24580
  1488.8 103.3 %copy-start.48 = (f32[256]{0:T(256)S(1)}, f32[256]{0:T(256)}, u32[]{:S(2)}) copy-start(f32[256]{0:T(256)} %copy-done.46) | copy-start | bytes 3076
  1488.8 103.3 %copy-start.54 = (f32[256]{0:T(256)S(1)}, f32[256]{0:T(256)}, u32[]{:S(2)}) copy-start(f32[256]{0:T(256)} %copy-done.53) | copy-start | bytes 3076
  1490.5 33.3 %collective-permute-start.1 = (bf16[256,2048]{1,0:T(8,128)(2,1)}, bf16[256,2048]{1,0:T(8,128)(2,1)}, u32[]{:S(2)}, u32[]{:S(2)}) collective-permute-start(bf16[256,2048]{1,0:T(8,128)(2,1)} %get-tuple-element.376), channel_id=1, source_target_pairs={{0,8},{4,12},{8,16},{12,20},{16,24},{20,28},{24,0},{28,4},{1,9},{5... | collective-permute-start | bytes 3145736 | tf_op jit(solution)/shard_map/ppermute | solution.py:288
  1499.8 46.6 %collective-permute-start.3 = (bf16[256,2048]{1,0:T(8,128)(2,1)}, bf16[256,2048]{1,0:T(8,128)(2,1)}, u32[]{:S(2)}, u32[]{:S(2)}) collective-permute-start(bf16[256,2048]{1,0:T(8,128)(2,1)} %get-tuple-element.377), channel_id=1, source_target_pairs={{0,24},{4,28},{8,0},{12,4},{16,8},{20,12},{24,16},{28,20},{1,25},{... | collective-permute-start | bytes 3145736 | tf_op jit(solution)/shard_map/ppermute | solution.py:288
  1499.8 92.3 %collective-permute-start.2 = (bf16[256,2048]{1,0:T(8,128)(2,1)}, bf16[256,2048]{1,0:T(8,128)(2,1)}, u32[]{:S(2)}, u32[]{:S(2)}) collective-permute-start(bf16[256,2048]{1,0:T(8,128)(2,1)} %get-tuple-element.378), channel_id=1, source_target_pairs={{0,16},{4,20},{8,24},{12,28},{16,0},{20,4},{24,8},{28,12},{1,17},{... | collective-permute-start | bytes 3145736 | tf_op jit(solution)/shard_map/ppermute | solution.py:288
  1506.9 93.5 %all-to-all-start.1 = ((bf16[8,64,3,256]{3,1,2,0:T(8,128)(2,1)}), bf16[8,64,3,256]{3,1,2,0:T(8,128)(2,1)}, u32[]{:S(2)}, u32[]{:S(2)}) async-start(bf16[8,64,3,256]{3,1,2,0:T(8,128)(2,1)} %copy.200), calls=%async_computation.2 | async-start | bytes 1572864 | tf_op jit(solution)/shard_map/all_to_all | solution.py:488
  1888.2 34.1 %copy-start.1 = (bf16[512,2048]{1,0:T(8,128)(2,1)S(1)}, bf16[512,2048]{1,0:T(8,128)(2,1)}, u32[]{:S(2)}) copy-start(bf16[512,2048]{1,0:T(8,128)(2,1)} %param.27) | copy-start | bytes 6291460
  (30 other events, 157.0 us)
Sparse Core Ops, SparseCore 0:
  11.0 31.2 all-gather.5
  43.8 58.2 all-gather.7
  103.7 105.9 all-gather.11
  211.7 105.8 all-gather.9
  319.0 105.8 all-gather.13
  1235.6 39.6 reduce-scatter.11
  1342.4 25.4 reduce-scatter.23
  1370.2 139.2 reduce-scatter.21
  1512.1 120.9 reduce-scatter.19
  1635.5 125.0 reduce-scatter.17
  1763.1 125.0 reduce-scatter.15
  1891.2 31.1 reduce-scatter.13

commit v2 on v1

v2 whole, which is shorter than its diff:
```python
import functools
import jax
import jax.numpy as jnp
from jax import lax
from jax.experimental import pallas as pl
from jax.experimental.pallas import tpu as pltpu
from jax.sharding import PartitionSpec as P

MESH = pl.DeviceIdType.MESH
ANY = pl.ANY
H = 16
epsilon = 1e-05


def work(us):
    return pl.CostEstimate(flops=int(us * 6e8), bytes_accessed=0, transcendentals=0)


def greet(peers):
    barrier = pltpu.get_barrier_semaphore()
    for peer in peers:
        pl.semaphore_signal(barrier, inc=1, device_id={"seq": peer}, device_id_type=MESH)
    pl.semaphore_wait(barrier, len(peers))


def push(src, dst, send, recv, peer):
    return pltpu.make_async_remote_copy(
        src_ref=src, dst_ref=dst, send_sem=send, recv_sem=recv,
        device_id={"seq": peer}, device_id_type=MESH)


def gather_kernel(n, pieces, own, out, send_sem, recv_sem, copy_sem):
    pair = 2
    lines = n // pair
    me = lax.axis_index("seq")
    a, b = me // pair, me % pair
    column = [((a + k) % lines) * pair + b for k in range(1, lines)]
    back = [((a + lines - k) % lines) * pair + b for k in range(1, lines)]
    across = a * pair + (1 - b)
    greet(column + [across])
    rows = own.shape[0] // pieces
    local = pltpu.make_async_copy(own, out.at[me], copy_sem)
    local.start()

    def piece(p):
        return pl.ds(p * rows, rows)

    sends = []
    for p in range(pieces):
        for k in range(lines):
            peer = across if k == 0 else column[k - 1]
            copy = push(own.at[piece(p)], out.at[me, piece(p)], send_sem.at[k, p], recv_sem.at[k, p], peer)
            copy.start()
            sends.append(copy)
    relays = []
    for p in range(pieces):
        for k in range(1, lines):
            src = back[k - 1]
            push(own.at[piece(p)], out.at[src, piece(p)], send_sem.at[k, p], recv_sem.at[k, p], across).wait_recv()
            slot = lines + k - 1
            copy = push(out.at[src, piece(p)], out.at[src, piece(p)], send_sem.at[slot, p], recv_sem.at[slot, p], across)
            copy.start()
            relays.append(copy)
    for p in range(pieces):
        push(own.at[piece(p)], out.at[across, piece(p)], send_sem.at[0, p], recv_sem.at[0, p], across).wait_recv()
    for copy in relays:
        copy.wait_recv()
    for copy in sends + relays:
        copy.wait_send()
    local.wait()


def gather_rows(x, n, pieces=4, collective_id=0):
    slots = n // 2 + n // 2 - 1
    return pl.pallas_call(
        functools.partial(gather_kernel, n, pieces),
        out_shape=jax.ShapeDtypeStruct((n,) + x.shape, x.dtype),
        in_specs=[pl.BlockSpec(memory_space=pltpu.VMEM)],
        out_specs=pl.BlockSpec(memory_space=ANY),
        scratch_shapes=[
            pltpu.SemaphoreType.DMA((slots, pieces)),
            pltpu.SemaphoreType.DMA((slots, pieces)),
            pltpu.SemaphoreType.DMA,
        ],
        compiler_params=pltpu.CompilerParams(collective_id=collective_id, has_side_effects=True),
        cost_estimate=work(105),
        name="gather_rows",
    )(x)


def reduce_kernel(n, pieces, part, out, mine, got, sums, landed, send_sem, recv_sem, load_sem):
    pair = 2
    lines = n // pair
    me = lax.axis_index("seq")
    a, b = me // pair, me % pair
    column = [((a + k) % lines) * pair + b for k in range(1, lines)]
    across = a * pair + (1 - b)
    greet(column + [across])
    rows = out.shape[0] // pieces
    order = list(range(1, lines)) + [0]

    def piece(p):
        return pl.ds(p * rows, rows)

    firsts, loads = {}, {}
    for k in order:
        line = (a + k) % lines
        for p in range(pieces):
            copy = push(part.at[line * pair + (1 - b), piece(p)], got.at[k, piece(p)],
                        send_sem.at[k, p], recv_sem.at[k, p], across)
            copy.start()
            firsts[k, p] = copy
            load = pltpu.make_async_copy(part.at[line * pair + b, piece(p)], mine.at[k, piece(p)], load_sem.at[k, p])
            load.start()
            loads[k, p] = load
    seconds = {}
    for k in order:
        for p in range(pieces):
            firsts[k, p].wait_recv()
            loads[k, p].wait()
            total = mine[k, piece(p)].astype(jnp.float32) + got[k, piece(p)].astype(jnp.float32)
            if k:
                sums[k - 1, piece(p)] = total.astype(jnp.bfloat16)
                slot = lines + k - 1
                copy = push(sums.at[k - 1, piece(p)], landed.at[k - 1, piece(p)],
                            send_sem.at[slot, p], recv_sem.at[slot, p], column[k - 1])
                copy.start()
                seconds[k, p] = copy
            else:
                for j in range(1, lines):
                    seconds[j, p].wait_recv()
                    total += landed[j - 1, piece(p)].astype(jnp.float32)
                out[piece(p), :] = total
    for copy in list(firsts.values()) + list(seconds.values()):
        copy.wait_send()


def reduce_rows(part, n, pieces=4, collective_id=1):
    _, rows, width = part.shape
    lines = n // 2
    slots = lines + lines - 1
    return pl.pallas_call(
        functools.partial(reduce_kernel, n, pieces),
        out_shape=jax.ShapeDtypeStruct((rows, width), jnp.float32),
        in_specs=[pl.BlockSpec(memory_space=ANY)],
        out_specs=pl.BlockSpec(memory_space=pltpu.VMEM),
        scratch_shapes=[
            pltpu.VMEM((lines, rows, width), jnp.bfloat16),
            pltpu.VMEM((lines, rows, width), jnp.bfloat16),
            pltpu.VMEM((lines - 1, rows, width), jnp.bfloat16),
            pltpu.VMEM((lines - 1, rows, width), jnp.bfloat16),
            pltpu.SemaphoreType.DMA((slots, pieces)),
            pltpu.SemaphoreType.DMA((slots, pieces)),
            pltpu.SemaphoreType.DMA((lines, pieces)),
        ],
        compiler_params=pltpu.CompilerParams(collective_id=collective_id, has_side_effects=True),
        cost_estimate=work(98),
        name="reduce_rows",
    )(part)


def gains_kernel(n, groups, sent, own, out, taken, summed, landed, send_sem, recv_sem, side_send, side_recv):
    me, group = lax.axis_index("seq"), lax.axis_index("fsdp")
    barrier = pltpu.get_barrier_semaphore()
    peers = [(me + k) % n for k in range(1, n)]
    mates = [(group + k) % groups for k in range(1, groups)]
    for peer in peers:
        pl.semaphore_signal(barrier, inc=1, device_id={"seq": peer}, device_id_type=MESH)
    for mate in mates:
        pl.semaphore_signal(barrier, inc=1, device_id={"fsdp": mate}, device_id_type=MESH)
    pl.semaphore_wait(barrier, n - 1 + groups - 1)
    copies = []
    for k in range(1, n):
        copy = push(sent.at[peers[k - 1]], taken.at[k - 1], send_sem.at[k - 1], recv_sem.at[k - 1], peers[k - 1])
        copy.start()
        copies.append(copy)
    total = sent[me] + own[...]
    for k in range(1, n):
        copies[k - 1].wait_recv()
        total = total + taken[k - 1]
    summed[...] = total
    sides = []
    for k in range(1, groups):
        side = pltpu.make_async_remote_copy(
            src_ref=summed, dst_ref=landed.at[k - 1], send_sem=side_send.at[k - 1], recv_sem=side_recv.at[k - 1],
            device_id={"fsdp": mates[k - 1]}, device_id_type=MESH)
        side.start()
        sides.append(side)
    for k in range(1, groups):
        sides[k - 1].wait_recv()
        total = total + landed[k - 1]
    out[...] = total
    for copy in copies + sides:
        copy.wait_send()


def sum_gains(sent, own, n, groups, collective_id):
    shape = own.shape
    return pl.pallas_call(
        functools.partial(gains_kernel, n, groups),
        out_shape=jax.ShapeDtypeStruct(shape, own.dtype),
        in_specs=[pl.BlockSpec(memory_space=pltpu.VMEM)] * 2,
        out_specs=pl.BlockSpec(memory_space=pltpu.VMEM),
        scratch_shapes=[
            pltpu.VMEM((n - 1,) + shape, own.dtype),
            pltpu.VMEM(shape, own.dtype),
            pltpu.VMEM((groups - 1,) + shape, own.dtype),
            pltpu.SemaphoreType.DMA((n - 1,)),
            pltpu.SemaphoreType.DMA((n - 1,)),
            pltpu.SemaphoreType.DMA((groups - 1,)),
            pltpu.SemaphoreType.DMA((groups - 1,)),
        ],
        compiler_params=pltpu.CompilerParams(collective_id=collective_id, has_side_effects=True),
        cost_estimate=work(10),
        name="sum_gains",
    )(sent, own)


def widen_kernel(x_ref, o_ref):
    for e in range(x_ref.shape[0]):
        o_ref[:, e, :] = x_ref[e].astype(jnp.float32)


def widen(x):
    experts, rows, columns = x.shape
    step = min(128, rows)
    return pl.pallas_call(
        widen_kernel,
        grid=(rows // step,),
        out_shape=jax.ShapeDtypeStruct((rows, experts, columns), jnp.float32),
        in_specs=[pl.BlockSpec((experts, step, columns), lambda i: (0, i, 0))],
        out_specs=pl.BlockSpec((step, experts, columns), lambda i: (i, 0, 0)),
        cost_estimate=work(5),
        name="widen",
    )(x)


def masked(block):
    keys = lax.broadcasted_iota(jnp.int32, (block, block), 0)
    rows = lax.broadcasted_iota(jnp.int32, (block, block), 1)
    return keys <= rows


def across_lanes(a, b):
    return lax.dot_general(a, b, (((1,), (1,)), ((), ())), preferred_element_type=jnp.float32)


def down_rows(a, b):
    return lax.dot_general(a, b, (((0,), (0,)), ((), ())), preferred_element_type=jnp.float32)


LOG2E = 1.4426950408889634


def attend_kernel(block, scale, q_ref, k_ref, v_ref, o_ref, lse_ref, s_ref, acc_ref):
    length, dim = q_ref.shape

    def rows(i):
        return pl.ds(pl.multiple_of(i * block, block), block)

    def one_block(i, _):
        q = q_ref[rows(i), :]
        diag = across_lanes(k_ref[rows(i), :], q) * (scale * LOG2E)
        diag = jnp.where(masked(block), diag, -1e30)
        s_ref[rows(i), :] = diag
        peak = jnp.max(diag, axis=0, keepdims=True)

        def score(j, peak):
            s = across_lanes(k_ref[rows(j), :], q) * (scale * LOG2E)
            s_ref[rows(j), :] = s
            return jnp.maximum(peak, jnp.max(s, axis=0, keepdims=True))

        peak = lax.fori_loop(0, i, score, peak)
        acc_ref[...] = jnp.zeros_like(acc_ref)

        def weigh(j, total):
            p = jnp.exp2(s_ref[rows(j), :] - peak)
            acc_ref[...] += down_rows(v_ref[rows(j), :], p.astype(jnp.bfloat16))
            return total + jnp.sum(p, axis=0, keepdims=True)

        total = lax.fori_loop(0, i + 1, weigh, jnp.zeros_like(peak))
        o_ref[rows(i), :] = (acc_ref[...] / total).T.astype(o_ref.dtype)
        lse_ref[0, :, rows(i)] = peak + jnp.log2(total)
        return 0

    lax.fori_loop(0, length // block, one_block, 0)


def attend(q, k, v, heads, block, scale):
    length, width = q.shape
    dim = width // heads
    spec = pl.BlockSpec((length, dim), lambda h: (0, h))
    return pl.pallas_call(
        functools.partial(attend_kernel, block, scale),
        grid=(heads,),
        out_shape=(
            jax.ShapeDtypeStruct(q.shape, q.dtype),
            jax.ShapeDtypeStruct((heads, 1, length), jnp.float32),
        ),
        in_specs=[spec] * 3,
        out_specs=[spec, pl.BlockSpec((1, 1, length), lambda h: (h, 0, 0))],
        scratch_shapes=[
            pltpu.VMEM((length, block), jnp.float32),
            pltpu.VMEM((dim, block), jnp.float32),
        ],
        cost_estimate=work(25),
        name="attend",
    )(q, k, v)


def attend_back_kernel(
    block, scale, q_ref, k_ref, v_ref, g_ref, o_ref, lse_ref, dq_ref, dk_ref, dv_ref, dk_acc, dv_acc, dq_acc
):
    length, dim = q_ref.shape
    dk_acc[...] = jnp.zeros_like(dk_acc)
    dv_acc[...] = jnp.zeros_like(dv_acc)

    def rows(i):
        return pl.ds(pl.multiple_of(i * block, block), block)

    def one_block(i, _):
        q, g = q_ref[rows(i), :], g_ref[rows(i), :]
        lse = lse_ref[0, :, rows(i)]
        products = g.astype(jnp.float32) * o_ref[rows(i), :].astype(jnp.float32)
        shift = lax.dot_general(
            jnp.ones((8, dim), jnp.float32), products, (((1,), (1,)), ((), ())),
            precision=lax.Precision.HIGHEST, preferred_element_type=jnp.float32,
        )[:1]

        def pair(j, keep):
            k, v = k_ref[rows(j), :], v_ref[rows(j), :]
            p = jnp.exp2(across_lanes(k, q) * (scale * LOG2E) - lse)
            if keep is not None:
                p = jnp.where(keep, p, 0.0)
            ds = (p * (across_lanes(v, g) - shift) * scale).astype(jnp.bfloat16)
            dv_acc[rows(j), :] += jnp.dot(p.astype(jnp.bfloat16), g, preferred_element_type=jnp.float32)
            dk_acc[rows(j), :] += jnp.dot(ds, q, preferred_element_type=jnp.float32)
            dq_acc[...] += down_rows(k, ds)

        dq_acc[...] = jnp.zeros_like(dq_acc)
        pair(i, masked(block))

        def body(j, _):
            pair(j, None)
            return 0

        lax.fori_loop(0, i, body, 0)
        dq_ref[rows(i), :] = dq_acc[...].T.astype(dq_ref.dtype)
        return 0

    lax.fori_loop(0, length // block, one_block, 0)
    dk_ref[...] = dk_acc[...].astype(dk_ref.dtype)
    dv_ref[...] = dv_acc[...].astype(dv_ref.dtype)


def attend_back(q, k, v, g, o, lse, heads, block, scale):
    length, width = q.shape
    dim = width // heads
    spec = pl.BlockSpec((length, dim), lambda h: (0, h))
    return pl.pallas_call(
        functools.partial(attend_back_kernel, block, scale),
        grid=(heads,),
        out_shape=(jax.ShapeDtypeStruct(q.shape, q.dtype),) * 3,
        in_specs=[spec] * 5 + [pl.BlockSpec((1, 1, length), lambda h: (h, 0, 0))],
        out_specs=[spec] * 3,
        scratch_shapes=[
            pltpu.VMEM((length, dim), jnp.float32),
            pltpu.VMEM((length, dim), jnp.float32),
            pltpu.VMEM((dim, block), jnp.float32),
        ],
        cost_estimate=work(60),
        name="attend_back",
    )(q, k, v, g, o, lse)


def project_kernel(
    n, groups, pieces, own, w_query, w_key, w_value, gain_own,
    normed, proj, squares, w_ref, gains, held, send_sem, recv_sem, side_send, side_recv, copy_sem
):
    pair = 2
    lines = n // pair
    me, group = lax.axis_index("seq"), lax.axis_index("fsdp")
    a, b = me // pair, me % pair
    column = [((a + k) % lines) * pair + b for k in range(1, lines)]
    back = [((a + lines - k) % lines) * pair + b for k in range(1, lines)]
    across = a * pair + (1 - b)
    mates = [(group + k) % groups for k in range(1, groups)]
    barrier = pltpu.get_barrier_semaphore()
    for peer in column + [across]:
        pl.semaphore_signal(barrier, inc=1, device_id={"seq": peer}, device_id_type=MESH)
    for mate in mates:
        pl.semaphore_signal(barrier, inc=1, device_id={"fsdp": mate}, device_id_type=MESH)
    pl.semaphore_wait(barrier, lines + groups - 1)
    rows, width = own.shape
    step = rows // pieces
    span = w_ref.shape[1] // 3
    shard = w_query.shape[0]

    def piece(p):
        return pl.ds(p * step, step)

    sends = []
    for p in range(pieces):
        for k in range(lines):
            peer = across if k == 0 else column[k - 1]
            copy = push(own.at[piece(p)], held.at[me, piece(p)], send_sem.at[k, p], recv_sem.at[k, p], peer)
            copy.start()
            sends.append(copy)

    shard_rows = pl.ds(pl.multiple_of(group * shard, shard), shard)
    mine = pl.ds(pl.multiple_of(me * span, span), span)
    blocks = [
        (w.at[:, mine], w_ref.at[shard_rows, part * span : (part + 1) * span])
        for part, w in enumerate((w_query, w_key, w_value))
    ]
    blocks.append((gain_own, gains.at[:, shard_rows]))
    locals_, sides = [], []
    for i, (src, dst) in enumerate(blocks):
        for k in range(1, groups):
            side = pltpu.make_async_remote_copy(
                src_ref=src, dst_ref=dst, send_sem=side_send.at[i, k - 1], recv_sem=side_recv.at[i, k - 1],
                device_id={"fsdp": mates[k - 1]}, device_id_type=MESH)
            side.start()
            sides.append(side)
        local = pltpu.make_async_copy(src, dst, copy_sem.at[i])
        local.start()
        locals_.append(local)
    for copy in locals_:
        copy.wait()
    for side in sides:
        side.wait_recv()

    def project(src, chunk):
        x = chunk[...].astype(jnp.float32)
        factor = lax.rsqrt(jnp.mean(x * x, axis=-1, keepdims=True) + epsilon)
        place = pl.ds(pl.multiple_of(src * rows, rows), rows)
        normed[place, :] = (x * factor * gains[0:1, :]).astype(jnp.bfloat16)
        for part in range(3):
            cols = slice(part * span, (part + 1) * span)
            out = jnp.dot(normed[place, :], w_ref[:, cols], preferred_element_type=jnp.float32)
            proj[place, cols] = out
            if part < 2:
                sums = lax.dot_general(
                    jnp.ones((8, span), jnp.float32), out * out, (((1,), (1,)), ((), ())),
                    precision=lax.Precision.HIGHEST, preferred_element_type=jnp.float32,
                )
                squares[pl.ds(part * n + src, 1), :] = sums[:1]

    relays = []
    for p in range(pieces):
        for k in range(1, lines):
            src = back[k - 1]
            push(own.at[piece(p)], held.at[src, piece(p)], send_sem.at[k, p], recv_sem.at[k, p], across).wait_recv()
            slot = lines + k - 1
            copy = push(held.at[src, piece(p)], held.at[src, piece(p)], send_sem.at[slot, p], recv_sem.at[slot, p], across)
            copy.start()
            relays.append(copy)
        if p == pieces // 2 - 1:
            project(me, own)
    for p in range(pieces):
        push(own.at[piece(p)], held.at[across, piece(p)], send_sem.at[0, p], recv_sem.at[0, p], across).wait_recv()
    project(across, held.at[across])
    for k in range(1, lines):
        project(back[k - 1], held.at[back[k - 1]])
    for k in range(1, lines):
        for p in range(pieces):
            relays[p * (lines - 1) + k - 1].wait_recv()
        src = ((a + lines - k) % lines) * pair + 1 - b
        project(src, held.at[src])
    for copy in sends + relays + sides:
        copy.wait_send()


def project_rows(x, w_query, w_key, w_value, gains, n, groups, pieces, collective_id):
    rows, width = x.shape
    span = w_query.shape[1] // n
    slots = n // 2 + n // 2 - 1
    vmem = pl.BlockSpec(memory_space=pltpu.VMEM)
    hbm = pl.BlockSpec(memory_space=ANY)
    return pl.pallas_call(
        functools.partial(project_kernel, n, groups, pieces),
        out_shape=(
            jax.ShapeDtypeStruct((n * rows, width), jnp.bfloat16),
            jax.ShapeDtypeStruct((n * rows, 3 * span), jnp.float32),
            jax.ShapeDtypeStruct((2 * n, rows), jnp.float32),
            jax.ShapeDtypeStruct((width, 3 * span), jnp.bfloat16),
            jax.ShapeDtypeStruct((8, width), jnp.float32),
        ),
        in_specs=[vmem, hbm, hbm, hbm, vmem],
        out_specs=[vmem] * 5,
        scratch_shapes=[
            pltpu.VMEM((n, rows, width), jnp.bfloat16),
            pltpu.SemaphoreType.DMA((slots, pieces)),
            pltpu.SemaphoreType.DMA((slots, pieces)),
            pltpu.SemaphoreType.DMA((4, groups - 1)),
            pltpu.SemaphoreType.DMA((4, groups - 1)),
            pltpu.SemaphoreType.DMA((4,)),
        ],
        compiler_params=pltpu.CompilerParams(
            collective_id=collective_id, has_side_effects=True, vmem_limit_bytes=50 << 20
        ),
        cost_estimate=work(110),
        name="project_rows",
    )(x, w_query, w_key, w_value, gains)


def as_columns(row, lanes):
    return jnp.broadcast_to(row, (lanes, row.shape[1])).T


def turn_tables(c, near_cos, near_sin, far_cos, far_sin):
    far_c, far_s = far_cos[pl.ds(c, 1), :], far_sin[pl.ds(c, 1), :]
    cosine = near_cos[...] * far_c - near_sin[...] * far_s
    sine = near_sin[...] * far_c + near_cos[...] * far_s
    first = lax.broadcasted_iota(jnp.int32, sine.shape, 1) < sine.shape[1] // 2
    return cosine, jnp.where(first, -sine, sine)


def add_over_seq(n, own, landed, send_sem, recv_sem, peers):
    copies = []
    for k in range(1, n):
        copy = push(own, landed.at[k - 1], send_sem.at[k - 1], recv_sem.at[k - 1], peers[k - 1])
        copy.start()
        copies.append(copy)
    return copies


def rotate_kernel(
    n, full, squares, sent, proj, gains, near_cos, near_sin, far_cos, far_sin,
    queries, keys, values, factors, taken, landed, send_sem, recv_sem, copy_sem
):
    me = lax.axis_index("seq")
    peers = [(me + k) % n for k in range(1, n)]
    greet(peers)
    local = pltpu.make_async_copy(sent.at[me], taken.at[me], copy_sem)
    local.start()
    copies = add_over_seq(n, squares, landed, send_sem.at[0], recv_sem.at[0], peers)
    swaps = []
    for k in range(1, n):
        swap = push(sent.at[peers[k - 1]], taken.at[me], send_sem.at[1, k - 1], recv_sem.at[1, k - 1], peers[k - 1])
        swap.start()
        swaps.append(swap)
    span = queries.shape[1]
    rows = squares.shape[1]
    lanes = near_cos.shape[1]
    total = squares[...]
    for k in range(1, n):
        copies[k - 1].wait_recv()
        total = total + landed[k - 1]
    factors[...] = lax.rsqrt(total / full + epsilon)

    def chunk(c, _):
        place = pl.ds(pl.multiple_of(c * rows, rows), rows)
        cosine, sine = turn_tables(c, near_cos, near_sin, far_cos, far_sin)
        for part, out in ((0, queries), (1, keys)):
            factor = as_columns(factors[pl.ds(part * n + c, 1), :], lanes)
            for h in range(span // lanes):
                cols = slice(part * span + h * lanes, part * span + (h + 1) * lanes)
                x = proj[place, cols] * factor * gains[part : part + 1, h * lanes : (h + 1) * lanes]
                turned = x * cosine + pltpu.roll(x, lanes // 2, 1) * sine
                out[place, h * lanes : (h + 1) * lanes] = turned.astype(jnp.bfloat16)
        values[place, :] = proj[place, 2 * span :].astype(jnp.bfloat16)
        return 0

    lax.fori_loop(0, n, chunk, 0)
    for copy in copies:
        copy.wait_send()
    for swap in swaps:
        swap.wait()
    local.wait()


def rotate_rows(squares, sent, proj, gains, tables, n, full, collective_id):
    length, outs = proj.shape
    span = outs // 3
    vmem = pl.BlockSpec(memory_space=pltpu.VMEM)
    heads = jax.ShapeDtypeStruct((length, span), jnp.bfloat16)
    return pl.pallas_call(
        functools.partial(rotate_kernel, n, full),
        out_shape=(
            heads, heads, heads,
            jax.ShapeDtypeStruct(squares.shape, jnp.float32),
            jax.ShapeDtypeStruct(sent.shape, sent.dtype),
        ),
        in_specs=[vmem] * 8,
        out_specs=[vmem] * 5,
        scratch_shapes=[
            pltpu.VMEM((n - 1,) + squares.shape, jnp.float32),
            pltpu.SemaphoreType.DMA((2, n - 1)),
            pltpu.SemaphoreType.DMA((2, n - 1)),
            pltpu.SemaphoreType.DMA,
        ],
        compiler_params=pltpu.CompilerParams(
            collective_id=collective_id, has_side_effects=True, vmem_limit_bytes=40 << 20
        ),
        cost_estimate=work(15),
        name="rotate_rows",
    )(squares, sent, proj, gains, *tables)


def heads_back_kernel(
    n, full, dq, dk, dv, proj, factors, gains, near_cos, near_sin, far_cos, far_sin,
    grads, gain_grads, sums, landed, send_sem, recv_sem
):
    me = lax.axis_index("seq")
    peers = [(me + k) % n for k in range(1, n)]
    greet(peers)
    span = dq.shape[1]
    rows = sums.shape[1]
    lanes = near_cos.shape[1]
    count = span // lanes

    def parts(c, part, h, grad):
        place = pl.ds(pl.multiple_of(c * rows, rows), rows)
        cosine, sine = turn_tables(c, near_cos, near_sin, far_cos, far_sin)
        g = grad[place, h * lanes : (h + 1) * lanes].astype(jnp.float32)
        up = g * cosine + pltpu.roll(g * sine, lanes // 2, 1)
        factor = as_columns(factors[pl.ds(part * n + c, 1), :], lanes)
        cols = slice(part * span + h * lanes, part * span + (h + 1) * lanes)
        normal = proj[place, cols] * factor
        weighted = up * gains[part : part + 1, h * lanes : (h + 1) * lanes]
        return place, cols, up, factor, normal, weighted

    def first(c, _):
        for part, grad in ((0, dq), (1, dk)):
            products = 0.0
            for h in range(count):
                _, _, up, _, normal, weighted = parts(c, part, h, grad)
                products = products + weighted * normal
            total = lax.dot_general(
                jnp.ones((8, lanes), jnp.float32), products, (((1,), (1,)), ((), ())),
                precision=lax.Precision.HIGHEST, preferred_element_type=jnp.float32,
            )
            sums[pl.ds(part * n + c, 1), :] = total[:1]
        return 0

    lax.fori_loop(0, n, first, 0)
    copies = add_over_seq(n, sums, landed, send_sem, recv_sem, peers)
    gain_grads[...] = jnp.zeros_like(gain_grads)

    def gain_sum(c, _):
        for part, grad in ((0, dq), (1, dk)):
            for h in range(count):
                _, _, up, _, normal, _ = parts(c, part, h, grad)
                cell = (slice(part + 2, part + 3), slice(h * lanes, (h + 1) * lanes))
                gain_grads[cell] += jnp.sum(up * normal, axis=0, keepdims=True)
        place = pl.ds(pl.multiple_of(c * rows, rows), rows)
        grads[place, 2 * span :] = dv[place, :]
        return 0

    lax.fori_loop(0, n, gain_sum, 0)
    total = sums[...]
    for k in range(1, n):
        copies[k - 1].wait_recv()
        total = total + landed[k - 1]
    landed[0] = total / full

    def last(c, _):
        for part, grad in ((0, dq), (1, dk)):
            mean = as_columns(landed[0, pl.ds(part * n + c, 1), :], lanes)
            for h in range(count):
                place, cols, _, factor, normal, weighted = parts(c, part, h, grad)
                grads[place, cols] = (factor * (weighted - normal * mean)).astype(jnp.bfloat16)
        return 0

    lax.fori_loop(0, n, last, 0)
    for copy in copies:
        copy.wait_send()


def heads_back(dq, dk, dv, proj, factors, gains, tables, n, full, collective_id):
    length, span = dq.shape
    vmem = pl.BlockSpec(memory_space=pltpu.VMEM)
    return pl.pallas_call(
        functools.partial(heads_back_kernel, n, full),
        out_shape=(
            jax.ShapeDtypeStruct((length, 3 * span), jnp.bfloat16),
            jax.ShapeDtypeStruct((8, span), jnp.float32),
        ),
        in_specs=[vmem] * 10,
        out_specs=[vmem] * 2,
        scratch_shapes=[
            pltpu.VMEM(factors.shape, jnp.float32),
            pltpu.VMEM((n - 1,) + factors.shape, jnp.float32),
            pltpu.SemaphoreType.DMA((n - 1,)),
            pltpu.SemaphoreType.DMA((n - 1,)),
        ],
        compiler_params=pltpu.CompilerParams(
            collective_id=collective_id, has_side_effects=True, vmem_limit_bytes=40 << 20
        ),
        cost_estimate=work(20),
        name="heads_back",
    )(dq, dk, dv, proj, factors, gains, *tables)


def turn_parts(rows, n, dim):
    half = dim // 2
    frequency = jnp.power(10000.0, -2.0 * jnp.arange(half, dtype=jnp.float32) / dim)
    frequency = jnp.concatenate([frequency, frequency])[None]
    near = jnp.arange(rows, dtype=jnp.float32)[:, None] * frequency
    far = (rows * jnp.arange(n)).astype(jnp.float32)[:, None] * frequency
    return jnp.cos(near), jnp.sin(near), jnp.cos(far), jnp.sin(far)


def inverse_norm(values):
    return lax.rsqrt(jnp.mean(values * values, axis=-1, keepdims=True) + epsilon)


def norm_backward(values, factor, gain, upstream):
    normal = values * factor
    weighted = upstream * gain
    gain_term = jnp.sum(upstream * normal, axis=0)
    back = factor * (weighted - normal * jnp.mean(weighted * normal, axis=-1, keepdims=True))
    return (back, gain_term)


def across_pairs(lines, pair):
    return [(a * pair + b, a * pair + 1 - b) for a in range(lines) for b in range(pair)]


def along_lines(lines, pair, k):
    return [(a * pair + b, (a + k) % lines * pair + b) for a in range(lines) for b in range(pair)]


def gather_column(x, n):
    lines = n // 2
    return [x] + [lax.ppermute(x, "seq", along_lines(lines, 2, k)) for k in range(1, lines)]


def gather_across(column, n):
    return [lax.ppermute(c, "seq", across_pairs(n // 2, 2)) for c in column]


def gather_join(column, other, n):
    lines = n // 2
    me = lax.axis_index("seq")
    a, b = me // 2, me % 2
    out = jnp.zeros((n,) + column[0].shape, column[0].dtype)
    for k in range(lines):
        line = (a + lines - k) % lines
        out = lax.dynamic_update_index_in_dim(out, column[k], line * 2 + b, 0)
        out = lax.dynamic_update_index_in_dim(out, other[k], line * 2 + 1 - b, 0)
    return out


def reduce_across(part, n):
    pair = 2
    b = lax.axis_index("seq") % pair
    halves = part.reshape(n // pair, pair, *part.shape[1:])
    give = lax.dynamic_index_in_dim(halves, 1 - b, 1, keepdims=False)
    keep = lax.dynamic_index_in_dim(halves, b, 1, keepdims=False)
    return keep, lax.ppermute(give, "seq", across_pairs(n // pair, pair))


def reduce_column(keep, got, n):
    lines = n // 2
    a = lax.axis_index("seq") // 2
    sums = (keep.astype(jnp.float32) + got.astype(jnp.float32)).astype(keep.dtype)
    pieces = [lax.dynamic_index_in_dim(sums, a, 0, keepdims=False)]
    for k in range(1, lines):
        piece = lax.dynamic_index_in_dim(sums, (a + k) % lines, 0, keepdims=False)
        pieces.append(lax.ppermute(piece, "seq", along_lines(lines, 2, k)))
    return pieces


def local(
    tokens, routes, route_weights, cotangent, attn_gain, query_gain, key_gain, ffn_gain,
    w_query, w_key, w_value, w_out, w_gate, w_up, w_down,
):
    n = lax.axis_size("seq")
    groups = lax.axis_size("fsdp")
    me = lax.axis_index("seq")
    width = tokens.shape[-1]
    own_tokens = tokens.reshape(-1, width)
    rows = own_tokens.shape[0]
    length = rows * n
    picks = routes.shape[-1]
    local_experts = w_gate.shape[1]
    experts = local_experts * n
    capacity = 3 * rows * picks // (2 * experts)
    head_dim = width // H
    heads = H // n
    span = heads * head_dim
    part = width // (n * groups)
    scale = head_dim ** (-0.5)
    bf, f32 = jnp.bfloat16, jnp.float32
    barrier = lax.optimization_barrier

    own_gains = jnp.stack([attn_gain, query_gain, key_gain, ffn_gain]).astype(f32)
    own_gains = jnp.pad(own_gains, ((0, 4), (0, 0)))
    full_out = lax.all_gather(w_out, "fsdp", axis=0, tiled=True)
    by_expert = lambda w: lax.all_gather(jnp.swapaxes(w, 0, 1), "fsdp", axis=1, tiled=True)
    full_gate = by_expert(w_gate)
    normed, proj, squares, w_heads, gains = project_rows(
        own_tokens, w_query, w_key, w_value, own_gains, n, groups, 8, 0
    )
    cot_own, w_up, w_down, squares = barrier((cotangent.reshape(rows, width), w_up, w_down, squares))
    full_up, full_down = by_expert(w_up), by_expert(w_down)
    cot_column = gather_column(cot_own, n)
    gain_attn, gain_ffn = gains[0], gains[3]
    head_gains = lax.dynamic_slice(gains, (1, me * span), (2, span))

    expert_ids = jnp.arange(experts, dtype=jnp.int32)
    named = routes.reshape(rows, picks)[None] == expert_ids[:, None, None]
    mixing = route_weights.reshape(rows, picks)[None]
    sent = jnp.sum(jnp.where(named, mixing, 0.0), axis=-1).reshape(n, local_experts, rows)
    tables = turn_parts(rows, n, head_dim)
    queries, keys, values, factors, weights = rotate_rows(
        squares, sent, proj, head_gains, tables, n, width, 1
    )
    block = min(512, length)
    heads_out, log_totals = attend(queries, keys, values, heads, block, scale)
    context = lax.all_to_all(heads_out, "seq", split_axis=0, concat_axis=1, tiled=True)
    inputs = own_tokens.astype(f32)
    mid = inputs + jnp.dot(context, full_out, preferred_element_type=f32)
    norm_two = inverse_norm(mid)
    ffn_in = (mid * norm_two * gain_ffn).astype(bf)

    ffn_all = gather_rows(ffn_in, n, 8, 2)
    cot_column, ffn_all = barrier((cot_column, ffn_all))
    cot_other = gather_across(cot_column, n)
    taken = weights > 0
    tri = (jnp.arange(rows)[:, None] <= jnp.arange(rows)[None, :]).astype(bf)
    rank = jnp.einsum("cet,tu->ceu", taken.astype(bf), tri, preferred_element_type=f32) - 1.0
    slot_ids = jnp.arange(capacity, dtype=f32)
    hit = (rank[:, :, None, :] == slot_ids[None, None, :, None]) & taken[:, :, None, :]
    place = hit.astype(bf)
    slot_weight = jnp.sum(jnp.where(hit, weights[:, :, None, :], 0.0), axis=-1)
    slot_weight = jnp.swapaxes(slot_weight, 0, 1)[..., None]
    place_rows = lambda v: jnp.einsum("cert,ctd->ecrd", place, v, preferred_element_type=f32)
    unplace = lambda v: jnp.einsum("cert,ecrd->ctd", place, v, preferred_element_type=f32).astype(bf)
    received = place_rows(ffn_all).astype(bf)
    gate = jnp.einsum("ecrd,edf->ecrf", received, full_gate, preferred_element_type=f32)
    up_part = jnp.einsum("ecrd,edf->ecrf", received, full_up, preferred_element_type=f32)
    sigmoid_gate = jax.nn.sigmoid(gate)
    activated = gate * sigmoid_gate
    hidden = (activated * up_part).astype(bf)
    expert_out = jnp.einsum("ecrf,edf->ecrd", hidden, full_down, preferred_element_type=f32)
    expert_out = (expert_out * slot_weight).astype(bf)
    ffn_part = unplace(expert_out)
    ffn_part, cot_other = barrier((ffn_part, cot_other))
    cot_all = gather_join(cot_column, cot_other, n)
    ffn_keep, ffn_got = reduce_across(ffn_part, n)

    out_grad = cotangent.reshape(rows, width).astype(f32)
    down_received = (place_rows(cot_all) * slot_weight).astype(bf)
    hidden_grad = jnp.einsum("ecrd,edf->ecrf", down_received, full_down, preferred_element_type=f32)
    slope = sigmoid_gate * (1.0 + gate * (1.0 - sigmoid_gate))
    gate_grad = (hidden_grad * up_part * slope).astype(bf)
    up_grad = (hidden_grad * activated).astype(bf)
    rows_grad = (
        jnp.einsum("ecrf,edf->ecrd", gate_grad, full_gate, preferred_element_type=f32)
        + jnp.einsum("ecrf,edf->ecrd", up_grad, full_up, preferred_element_type=f32)
    ).astype(bf)
    term = lambda a, b: jnp.einsum("ecrd,ecrf->edf", a, b, preferred_element_type=f32).astype(bf)
    scatter = lambda v: lax.psum_scatter(v, "fsdp", scatter_dimension=1, tiled=True)
    rows_part, ffn_keep, ffn_got, down_term, gate_term, up_term = barrier(
        (
            unplace(rows_grad),
            ffn_keep,
            ffn_got,
            term(down_received, hidden),
            term(received, gate_grad),
            term(received, up_grad),
        )
    )
    scattered = [scatter(down_term), scatter(gate_term), scatter(up_term)]
    ffn_in_grad = reduce_rows(rows_part, n, 8, 4)
    mid_back, ffn_gain_term = norm_backward(mid, norm_two, gain_ffn, ffn_in_grad)
    mid_grad = out_grad + mid_back
    branch_grad = mid_grad.astype(bf)

    branch_all = gather_rows(branch_grad, n, 8, 5).reshape(length, width)
    branch_all, ffn_keep, ffn_got = barrier((branch_all, ffn_keep, ffn_got))
    ffn_pieces = reduce_column(ffn_keep, ffn_got, n)
    out_rows = lax.dynamic_slice_in_dim(full_out, me * span, span, 0)
    heads_grad = jnp.einsum("te,de->td", branch_all, out_rows, preferred_element_type=f32).astype(bf)
    out_term = jnp.einsum("td,te->de", heads_out, branch_all, preferred_element_type=f32).astype(bf)
    query_back, key_back, value_back = attend_back(
        queries, keys, values, heads_grad, heads_out, log_totals, heads, block, scale
    )
    proj_grad, gain_terms = heads_back(
        query_back, key_back, value_back, proj, factors, head_gains, tables, n, width, 6
    )
    normed_part = jnp.einsum("te,de->td", proj_grad, w_heads, preferred_element_type=f32).astype(bf)
    head_term = jnp.einsum("td,te->de", normed, proj_grad, preferred_element_type=f32).astype(bf)
    head_term = head_term.reshape(n, groups, part, 3 * span).swapaxes(0, 1)
    normed_part, ffn_pieces, out_term, head_term, down_sum, gate_sum = barrier(
        (normed_part, ffn_pieces, out_term, head_term, *scattered[:2])
    )
    block_out = mid + sum(piece.astype(f32) for piece in ffn_pieces)
    out_sum = lax.psum_scatter(out_term, "fsdp", scatter_dimension=0, tiled=True).astype(f32)
    gate_sum, down_sum = widen(gate_sum), widen(down_sum)
    normed_grad = reduce_rows(normed_part.reshape(n, rows, width), n, 8, 7)
    input_back, attn_gain_term = norm_backward(inputs, inverse_norm(inputs), gain_attn, normed_grad)
    tokens_grad = mid_grad + input_back
    head_term, up_sum = barrier((head_term, scattered[2]))
    up_sum = widen(up_sum)
    head_term = lax.psum_scatter(head_term, "fsdp", scatter_dimension=0, tiled=True)
    head_term = head_term.reshape(n, part, 3, span)
    head_term = lax.all_to_all(head_term, "seq", split_axis=0, concat_axis=0, tiled=True)
    head_sums = [
        head_term[:, :, i].swapaxes(0, 1).reshape(part, width).astype(f32) for i in range(3)
    ]
    by_span = lambda v: v.reshape(n, 1, span)
    sent_gains = jnp.concatenate([by_span(attn_gain_term), by_span(ffn_gain_term)], axis=1)
    sent_gains = jnp.pad(sent_gains, ((0, 0), (0, 6), (0, 0)))
    gain_sums = sum_gains(sent_gains, gain_terms, n, groups, 8)
    gain_sums = lax.dynamic_slice_in_dim(gain_sums, lax.axis_index("fsdp") * part, part, 1)
    return (
        block_out.astype(bf).reshape(tokens.shape),
        tokens_grad.reshape(tokens.shape),
        gain_sums[0],
        gain_sums[2],
        gain_sums[3],
        gain_sums[1],
        head_sums[0],
        head_sums[1],
        head_sums[2],
        out_sum,
        gate_sum,
        up_sum,
        down_sum,
    )


def solution(mesh):
    rows3 = P("fsdp", "seq", None)
    both = P(("seq", "fsdp"))
    both2 = P(("seq", "fsdp"), None)
    placed = (rows3,) * 4 + (P("fsdp"),) * 4 + (P("fsdp", None),) * 4 + (rows3,) * 3
    return jax.shard_map(
        local,
        mesh=mesh,
        in_specs=placed,
        out_specs=(rows3,) * 2 + (both,) * 4 + (both2,) * 4 + (rows3,) * 3,
        check_vma=False,
    )
```

time: 1940 us -> 1310 us (0.68)
  waiting for transfers between devices: 533 us -> 104 us
  matrix products: 504 us -> 292 us
  Pallas kernels: 568 us -> 752 us
  other arithmetic: 107 us -> 27.9 us
  local copies, waits for them, and re-layouts: 151 us -> 75.2 us
    ppermute x11, waiting for transfers between devices: 261 us -> 1.69 us  [the longest x1 1.66 us: reduce_across(): return (keep, lax.ppermute(give, 'seq', across_pairs(n // pair, pair)))]
    pallas_call x2 -> x9, Pallas kernels: 43.8 us -> 290 us  [the longest x1 154 us: project_rows(): pl.pallas_call(functools.partial(project_kernel, n, groups, pieces), out_...]
    dot_general x30 -> x1, matrix products: 212 us -> 3.32 us  [local(): jnp.einsum('td,te->de', heads_out, branch_all, preferred_element_type=f32)]
    reduce_scatter x4, waiting for transfers between devices: 240 us -> 31.6 us  [the longest x3 31.6 us: local(): lax.psum_scatter(v, 'fsdp', scatter_dimension=1, tiled=True)]
    pallas_call x3 -> x2, Pallas kernels: 333 us -> 261 us  [gather_rows(): pl.pallas_call(functools.partial(gather_kernel, n, pieces), out_shape=jax...]
    unnamed x138 -> x123, local copies, waits for them, and re-layouts: 84.2 us -> 21.8 us
    all_to_all x1, waiting for transfers between devices: 12 us -> 63.9 us  [local(): lax.all_to_all(heads_out, 'seq', split_axis=0, concat_axis=1, tiled=True)]
    transpose x3 -> x0, other arithmetic: 20 us -> none  [local(): jnp.swapaxes(lax.psum_scatter(v, 'fsdp', scatter_dimension=1, tiled=True)...]
  transfers between devices with their start and end apart: 25 -> 22, of which waited for: 13 -> 4; matrix products, arithmetic and copies ran while one was open for 18% -> 21% of each run, Pallas kernels for 18% -> 58%
where the time goes in v2:
time: 1310 us; the launch traced here: 1290 us
  Pallas kernels  752 us (57%)
  matrix products  292 us (22%)
  waiting for transfers between devices  104 us (8%)
  local copies, waits for them, and re-layouts  75.2 us (6%)
  other arithmetic  27.9 us (2%)
  starting transfers between devices  26.7 us (2%)
  between operations  15 us (1%)
    pallas_call x2, Pallas kernels, gather_rows(): pl.pallas_call(functools.partial(gather_kernel, n, pieces), out_shape=jax...  261 us
    pallas_call x2, Pallas kernels, reduce_rows(): pl.pallas_call(functools.partial(reduce_kernel, n, pieces), out_shape=jax...  200 us
    pallas_call x1, Pallas kernels, project_rows(): pl.pallas_call(functools.partial(project_kernel, n, groups, pieces), out_...  154 us
    all_to_all x1, waiting for transfers between devices, local(): lax.all_to_all(heads_out, 'seq', split_axis=0, concat_axis=1, tiled=True)  63.9 us
    dot_general x3, matrix products, local(): jnp.einsum('ecrd,ecrf->edf', a, b, preferred_element_type=f32).astype(bf)  58.8 us
    pallas_call x1, Pallas kernels, heads_back(): pl.pallas_call(functools.partial(heads_back_kernel, n, full), out_shape=(...  57.5 us
    dot_general x2, matrix products, local(): jnp.einsum('cert,ecrd->ctd', place, v, preferred_element_type=f32)  34.2 us
    reduce_scatter x3, waiting for transfers between devices, local(): lax.psum_scatter(v, 'fsdp', scatter_dimension=1, tiled=True)  31.6 us
  transfers between devices with their start and end apart: 22, of which 4 were waited for; matrix products, arithmetic and copies ran while one was open for 21% of the time, Pallas kernels for 58%

profile of v2, /device:TPU:0, one launch (start us, length us, event | category | flops | bytes accessed | tf_op | source)
XLA Modules:
  0.0 1293.3 jit_solution(10082621911203125948)
XLA Ops:
  8.0 5.7 copy.160
  14.0 154.4 %project_rows.1 = (bf16[2048,2048]{1,0:T(8,128)(2,1)}, f32[2048,768]{1,0:T(8,128)}, f32[16,256]{1,0:T(8,128)S(1)}, bf16[2048,768]{1,0:T(8,128)(2,1)}, f32[8,2048]{1,0:T(8,128)S(1)}) custom-call(bf16[256,2048]{1,0:T(8,128)(2,1)S(1)} %bitcast.178, bf16[512,2048]{1,0:T(8,128)(2,1)S(1)} %copy-done.13, bf16[512,2048]{1,0:T(8,128)(2,1)} %w_key.1, ...), custom_call_target="tpu_custom_call" | custom-call | flops 65999998976 | tf_op jit(solution)/shard_map/project_rows/pallas_call | solution.py:480
  168.4 3.4 copy.159
  171.9 5.7 copy.158
  178.5 2.9 copy-done.14
  181.4 9.5 rotate_rows.1
  194.0 16.0 %attend.1 = (bf16[2048,256]{1,0:T(8,128)(2,1)}, f32[2,1,2048]{2,1,0:T(1,128)}) custom-call(bf16[2048,256]{1,0:T(8,128)(2,1)} %copy-done.16, bf16[2048,256]{1,0:T(8,128)(2,1)} %copy-done.17, bf16[2048,256]{1,0:T(8,128)(2,1)} %copy-done.18), custom_call_target="tpu_custom_call" | custom-call | flops 15000000512 | tf_op jit(solution)/shard_map/attend/pallas_call | solution.py:293
  209.9 2.3 copy.100
  212.2 4.2 all-to-all-start
  216.4 2.0 collective-permute-start
  218.4 2.4 collective-permute-start.1
  224.5 63.9 %all-to-all-done = bf16[8,256,256]{1,2,0:T(8,128)(2,1)S(1)} async-done(((bf16[8,256,256]{1,2,0:T(8,128)(2,1)}), bf16[8,256,256]{1,2,0:T(8,128)(2,1)S(1)}, u32[]{:S(2)}, u32[]{:S(2)}) %all-to-all-start) | async-done | bytes 1048608 | tf_op jit(solution)/shard_map/all_to_all | solution.py:813
  288.4 5.8 multiply_reduce_fusion.2
  296.8 150.0 %gather_rows.2 = bf16[8,256,2048]{2,1,0:T(8,128)(2,1)} custom-call(bf16[256,2048]{1,0:T(8,128)(2,1)} %multiply_convert_fusion.7.own), custom_call_target="tpu_custom_call" | custom-call | flops 62999998464 | tf_op jit(solution)/shard_map/gather_rows/pallas_call | solution.py:75
  446.9 2.0 collective-permute-start.4
  449.0 1.9 collective-permute-start.6
  451.0 4.5 broadcast_in_dim.72
  456.5 9.9 convert_bitcast_fusion
  466.4 22.6 %fusion.5 = f32[4,8,96,1024]{3,2,1,0:T(8,128)} fusion(bf16[4,2048,1024]{2,1,0:T(8,128)(2,1)} %all-gather.7.cloned.1.call-done, bf16[4,8,96,2048]{3,2,0,1:T(8,128)(2,1)} %convert_bitcast_fusion), kind=kOutput, calls=%fused_computation.11 | convolution fusion | flops 12884901888 | bytes 41943040 | tf_op jit(solution)/shard_map/ecrd,edf->ecrf/dot_general | solution.py:833
  489.0 26.6 %multiply_convert_fusion.4 = (bf16[4,8,96,1024]{3,2,1,0:T(8,128)(2,1)}, f32[4,8,96,1024]{3,2,1,0:T(8,128)}) fusion(f32[4,8,96,1024]{3,2,1,0:T(8,128)} %fusion.5, bf16[4,2048,1024]{2,1,0:T(8,128)(2,1)} %all-gather.9.cloned.1.call-done, bf16[4,8,96,2048]{3,2,0,1:T(8,128)(2,1)} %convert_bitcast_fusion), kind=kOutput, calls=%fused_computation.27 | convolution fusion | flops 12903776256 | bytes 60817408 | tf_op jit(solution)/shard_map/ecrd,edf->ecrf/dot_general | solution.py:834
  515.6 22.0 %fusion.7 = f32[4,8,96,2048]{3,2,0,1:T(8,128)} fusion(bf16[4,2048,1024]{2,1,0:T(8,128)(2,1)} %all-gather.11.cloned.1.call-done, bf16[4,8,96,1024]{3,2,1,0:T(8,128)(2,1)} %get-tuple-element.144), kind=kOutput, calls=%fused_computation.15 | convolution fusion | flops 12884901888 | bytes 48234496 | tf_op jit(solution)/shard_map/ecrf,edf->ecrd/dot_general | solution.py:838
  537.6 12.9 bitcast_convert_fusion.4
  550.5 2.3 bitcast_dynamic-update-slice_fusion.6
  552.8 2.3 bitcast_dynamic-update-slice_fusion.5
  555.1 2.3 bitcast_dynamic-update-slice_fusion.4
  557.4 2.3 bitcast_dynamic-update-slice_fusion.3
  560.8 2.3 bitcast_dynamic-update-slice_fusion.1
  564.2 9.9 fusion
  574.0 19.6 %bitcast_convert_fusion.2 = bf16[4,2048,1024]{2,1,0:T(8,128)(2,1)} fusion(bf16[4,8,96,2048]{3,2,0,1:T(8,128)(2,1)} %fusion, bf16[4,8,96,1024]{3,2,1,0:T(8,128)(2,1)} %get-tuple-element.144), kind=kOutput, calls=%fused_computation.2 | convolution fusion | flops 12893290496 | bytes 35651584 | tf_op jit(solution)/shard_map/ecrd,ecrf->edf/dot_general | solution.py:855
  593.6 29.2 %multiply_convert_fusion.2 = (bf16[4,8,96,1024]{3,2,1,0:T(8,128)(2,1)}, bf16[4,8,96,1024]{3,2,1,0:T(8,128)(2,1)}) fusion(f32[4,8,96,1024]{3,2,1,0:T(8,128)} %fusion.5, f32[4,8,96,1024]{3,2,1,0:T(8,128)} %get-tuple-element.145, bf16[4,2048,1024]{2,1,0:T(8,128)(2,1)} %all-gather.11.cloned.1.call-done, bf16[4,8,96,2048]{3,2,0,1:T(8,128)(2,1)} %fusion), kind=kOutput, calls=%fused_computation.24 | convolution fusion | flops 12925796352 | bytes 67108864 | tf_op jit(solution)/shard_map/ecrd,edf->ecrf/dot_general | solution.py:847
  622.8 19.6 %bitcast_convert_fusion = bf16[4,2048,1024]{2,1,0:T(8,128)(2,1)} fusion(bf16[4,8,96,2048]{3,2,0,1:T(8,128)(2,1)} %convert_bitcast_fusion, bf16[4,8,96,1024]{3,2,1,0:T(8,128)(2,1)} %get-tuple-element.119), kind=kOutput, calls=%fused_computation | convolution fusion | flops 12893290496 | bytes 35651584 | tf_op jit(solution)/shard_map/ecrd,ecrf->edf/dot_general | solution.py:855
  642.4 8.5 dynamic-slice_bitcast_fusion
  651.0 22.1 %fusion.9 = f32[4,8,96,2048]{3,2,0,1:T(8,128)} fusion(bf16[4,2048,1024]{2,1,0:T(8,128)(2,1)} %all-gather.9.cloned.1.call-done, bf16[4,8,96,1024]{3,2,1,0:T(8,128)(2,1)} %get-tuple-element.119), kind=kOutput, calls=%fused_computation.17 | convolution fusion | flops 12884901888 | bytes 48234496 | tf_op jit(solution)/shard_map/ecrf,edf->ecrd/dot_general | solution.py:853
  673.1 24.4 %fusion.11 = f32[4,8,96,2048]{3,2,0,1:T(8,128)} fusion(bf16[4,2048,1024]{2,1,0:T(8,128)(2,1)} %all-gather.7.cloned.1.call-done, bf16[4,8,96,1024]{3,2,1,0:T(8,128)(2,1)S(1)} %bitcast.215), kind=kOutput, calls=%fused_computation.19 | convolution fusion | flops 12884901888 | bytes 48234496 | tf_op jit(solution)/shard_map/ecrf,edf->ecrd/dot_general | solution.py:852
  697.5 21.3 %bitcast_convert_fusion.3.part = bf16[8,256,2048]{2,1,0:T(8,128)(2,1)} fusion(f32[4,8,96,2048]{3,2,0,1:T(8,128)} %fusion.11, f32[4,8,96,2048]{3,2,0,1:T(8,128)} %fusion.9, f32[8,4,256]{2,1,0:T(4,128)S(1)} %copy-done.33, pred[8,4,256]{2,1,0:T(4,128)(4,1)S(1)} %copy-done.35), kind=kOutput, calls=%fused_computation.13 | convolution fusion | flops 3239575552 | bytes 58761216 | tf_op jit(solution)/shard_map/cert,ecrd->ctd/dot_general | solution.py:831
  718.8 19.6 %bitcast_convert_fusion.1 = bf16[4,2048,1024]{2,1,0:T(8,128)(2,1)} fusion(bf16[4,8,96,2048]{3,2,0,1:T(8,128)(2,1)} %convert_bitcast_fusion, bf16[4,8,96,1024]{3,2,1,0:T(8,128)(2,1)S(1)} %bitcast.215), kind=kOutput, calls=%fused_computation.1 | convolution fusion | flops 12893290496 | bytes 35651584 | tf_op jit(solution)/shard_map/ecrd,ecrf->edf/dot_general | solution.py:855
  742.8 99.5 %reduce_rows.2 = f32[256,2048]{1,0:T(8,128)} custom-call(bf16[8,256,2048]{2,1,0:T(8,128)(2,1)} %bitcast_convert_fusion.3.part), custom_call_target="tpu_custom_call" | custom-call | flops 58800001024 | tf_op jit(solution)/shard_map/reduce_rows/pallas_call | solution.py:142
  842.3 2.7 multiply_reduce_fusion
  845.6 3.3 fusion.70.own
  848.9 111.3 %gather_rows.3 = bf16[8,256,2048]{2,1,0:T(8,128)(2,1)} custom-call(bf16[256,2048]{1,0:T(8,128)(2,1)} %fusion.70.own), custom_call_target="tpu_custom_call" | custom-call | flops 62999998464 | tf_op jit(solution)/shard_map/gather_rows/pallas_call | solution.py:75
  960.2 5.8 add_convert_fusion.2
  966.1 2.1 dynamic-slice_bitcast_fusion.2
  968.2 6.5 collective-permute-start.10
  975.3 4.7 convolution_convert_fusion.3.g_ref
  980.0 22.3 %attend_back.1 = (bf16[2048,256]{1,0:T(8,128)(2,1)}, bf16[2048,256]{1,0:T(8,128)(2,1)}, bf16[2048,256]{1,0:T(8,128)(2,1)}) custom-call(bf16[2048,256]{1,0:T(8,128)(2,1)} %copy-done.16, bf16[2048,256]{1,0:T(8,128)(2,1)} %copy-done.17, bf16[2048,256]{1,0:T(8,128)(2,1)} %copy-done.18, bf16[2048,256]{1,0:T(8,128)(2,1)} %convolution_convert_fusion.3.g_ref, ...), custom_call_target="tpu_custom_call" | custom-call | flops 35999997952 | tf_op jit(solution)/shard_map/attend_back/pallas_call | solution.py:360
  1002.4 3.5 copy-done.15
  1010.4 57.5 %heads_back.1 = (bf16[2048,768]{1,0:T(8,128)(2,1)S(1)}, f32[8,256]{1,0:T(8,128)S(1)}) custom-call(bf16[2048,256]{1,0:T(8,128)(2,1)S(1)} %copy-done.19, bf16[2048,256]{1,0:T(8,128)(2,1)S(1)} %copy-done.20, bf16[2048,256]{1,0:T(8,128)(2,1)S(1)} %copy-done.21, f32[2048,768]{1,0:T(8,128)S(1)} %copy-done.15, f32[16,256]{1,0:T(8,128)S(1)} %get-tuple-element.94.factors, ...), custom_call_target="tpu_custom_call" | custom-call | flops 12000000000 | tf_op jit(solution)/shard_map/heads_back/pallas_call | solution.py:674
  1068.0 9.4 convolution_convert_fusion.1
  1077.4 9.0 convolution_convert_fusion
  1086.4 2.0 copy.161
  1088.4 3.3 convolution_convert_fusion.2
  1091.8 31.6 %reduce-scatter.10.cloned.1.call-done.x_ref = bf16[4,512,1024]{2,1,0:T(8,128)(2,1)} async-done(((bf16[4,2048,1024]{2,1,0:T(8,128)(2,1)}), bf16[4,512,1024]{2,1,0:T(8,128)(2,1)}) %reduce-scatter.10.cloned.1.call-update) | async-done | bytes 4194320 | tf_op jit(solution)/shard_map/reduce_scatter | solution.py:856
  1123.6 100.9 %reduce_rows.3 = f32[256,2048]{1,0:T(8,128)} custom-call(bf16[8,256,2048]{2,1,0:T(8,128)(2,1)} %bitcast.213), custom_call_target="tpu_custom_call" | custom-call | flops 58800001024 | tf_op jit(solution)/shard_map/reduce_rows/pallas_call | solution.py:142
  1224.6 2.3 fusion.44
  1226.8 6.5 widen.4
  1233.4 6.5 widen.3
  1240.6 11.1 sum_gains.1
  1251.8 3.4 reshape.126
  1255.1 2.5 copy.116
  1257.6 4.6 all-to-all-start.1
  1263.5 6.5 widen.5
  1270.1 5.8 fusion.43
  1275.9 1.8 convert_element_type.183
  1277.7 5.1 all-to-all-done.1
  (200 shorter events, 30.5 us)
Async XLA Ops:
  7.2 6.7 copy-start
  7.2 281.2 %all-gather.5.cloned.1.call-start = ((), (), s32[]{:S(2)}) async-start(), calls=%async_computation.7 | async-start | bytes 10485760 | tf_op jit(solution)/shard_map/all_gather | solution.py:791
  8.0 458.4 %all-gather.7.cloned.1.call-start = ((), (), s32[]{:S(2)}) async-start(), calls=%async_computation.8 | async-start | bytes 20971520 | tf_op jit(solution)/shard_map/all_gather | solution.py:792
  13.8 475.2 %all-gather.9.cloned.1.call-start = ((), (), s32[]{:S(2)}) async-start(), calls=%async_computation.9 | async-start | bytes 20971520 | tf_op jit(solution)/shard_map/all_gather | solution.py:792
  14.0 154.4 %copy-start.29 = (bf16[512,4,1024]{2,1,0:T(4,128)(2,1)S(1)}, bf16[512,4,1024]{2,1,0:T(4,128)(2,1)}, u32[]{:S(2)}) copy-start(bf16[512,4,1024]{2,1,0:T(4,128)(2,1)} %param.28) | copy-start | bytes 12582916
  171.8 343.7 %all-gather.11.cloned.1.call-start = ((), (), s32[]{:S(2)}) async-start(), calls=%async_computation.10 | async-start | bytes 20971520 | tf_op jit(solution)/shard_map/all_gather | solution.py:792
  177.9 13.0 %copy-start.11 = (f32[2,256]{1,0:T(2,128)}, f32[2,256]{1,0:T(2,128)S(1)}, u32[]{:S(2)}) copy-start(f32[2,256]{1,0:T(2,128)S(1)} %constant_dynamic-slice_fusion.1.gains) | copy-start | bytes 6148
  178.0 12.9 %copy-start.7 = (f32[8,128]{1,0:T(8,128)}, f32[8,128]{1,0:T(8,128)S(1)}, u32[]{:S(2)}) copy-start(f32[8,128]{1,0:T(8,128)S(1)} %get-tuple-element.138.far_sin) | copy-start | bytes 12292
  178.0 12.9 %copy-start.9 = (f32[8,128]{1,0:T(8,128)}, f32[8,128]{1,0:T(8,128)S(1)}, u32[]{:S(2)}) copy-start(f32[8,128]{1,0:T(8,128)S(1)} %get-tuple-element.139.far_cos) | copy-start | bytes 12292
  178.5 12.4 copy-start.3
  178.5 12.4 copy-start.5
  193.9 22.4 %copy-start.26 = (bf16[1,256,2048]{2,1,0:T(8,128)(2,1)S(1)}, bf16[1,256,2048]{2,1,0:T(8,128)(2,1)}, u32[]{:S(2)}) copy-start(bf16[1,256,2048]{2,1,0:T(8,128)(2,1)} %param.18) | copy-start | bytes 3145732
  212.2 76.3 %all-to-all-start = ((bf16[8,256,256]{1,2,0:T(8,128)(2,1)}), bf16[8,256,256]{1,2,0:T(8,128)(2,1)S(1)}, u32[]{:S(2)}, u32[]{:S(2)}) async-start(bf16[8,256,256]{1,2,0:T(8,128)(2,1)} %copy.100), calls=%async_computation | async-start | bytes 2097152 | tf_op jit(solution)/shard_map/all_to_all | solution.py:813
  216.3 875.4 %reduce-scatter.6.cloned.1.call-start = ((), (), s32[]{:S(2)}) async-start(), calls=%async_computation.11 | async-start | bytes 20971520 | tf_op jit(solution)/shard_map/reduce_scatter | solution.py:856
  216.4 230.5 %collective-permute-start = (bf16[256,2048]{1,0:T(8,128)(2,1)S(1)}, bf16[256,2048]{1,0:T(8,128)(2,1)}, u32[]{:S(2)}, u32[]{:S(2)}) collective-permute-start(bf16[256,2048]{1,0:T(8,128)(2,1)S(1)} %bitcast.190), channel_id=1, source_target_pairs={{0,8},{4,12},{8,16},{12,20},{16,24},{20,28},{24,0},{28,4},{1,9},{5... | collective-permute-start | bytes 3145736 | tf_op jit(solution)/shard_map/ppermute | solution.py:727
  218.4 228.4 %collective-permute-start.1 = (bf16[256,2048]{1,0:T(8,128)(2,1)S(1)}, bf16[256,2048]{1,0:T(8,128)(2,1)}, u32[]{:S(2)}, u32[]{:S(2)}) collective-permute-start(bf16[256,2048]{1,0:T(8,128)(2,1)S(1)} %bitcast.191), channel_id=1, source_target_pairs={{0,16},{4,20},{8,24},{12,28},{16,0},{20,4},{24,8},{28,12},{1,17},{... | collective-permute-start | bytes 3145736 | tf_op jit(solution)/shard_map/ppermute | solution.py:727
  220.8 226.1 %collective-permute-start.2 = (bf16[256,2048]{1,0:T(8,128)(2,1)S(1)}, bf16[256,2048]{1,0:T(8,128)(2,1)}, u32[]{:S(2)}, u32[]{:S(2)}) collective-permute-start(bf16[256,2048]{1,0:T(8,128)(2,1)S(1)} %bitcast.192), channel_id=1, source_target_pairs={{0,24},{4,28},{8,0},{12,4},{16,8},{20,12},{24,16},{28,20},{1,25},{... | collective-permute-start | bytes 3145736 | tf_op jit(solution)/shard_map/ppermute | solution.py:727
  222.3 341.9 %copy-start.34 = (pred[8,4,256]{2,1,0:T(4,128)(4,1)}, pred[8,4,256]{2,1,0:T(4,128)(4,1)S(1)}, u32[]{:S(2)}) copy-start(pred[8,4,256]{2,1,0:T(4,128)(4,1)S(1)} %broadcast_compare_fusion) | copy-start | bytes 24580
  222.4 341.7 %copy-start.32 = (f32[8,4,256]{2,1,0:T(4,128)}, f32[8,4,256]{2,1,0:T(4,128)S(1)}, u32[]{:S(2)}) copy-start(f32[8,4,256]{2,1,0:T(4,128)S(1)} %copy.102) | copy-start | bytes 98308
  224.5 72.3 %copy-start.36 = (f32[1,2048]{1,0:T(1,128)}, f32[1,2048]{1,0:T(1,128)S(1)}, u32[]{:S(2)}) copy-start(f32[1,2048]{1,0:T(1,128)S(1)} %get-tuple-element.133) | copy-start | bytes 24580
  294.3 152.5 %copy-start.42 = (f32[256]{0:T(256)}, f32[256]{0:T(256)S(1)}, u32[]{:S(2)}) copy-start(f32[256]{0:T(256)S(1)} %add_rsqrt_fusion.1) | copy-start | bytes 3076
  446.9 103.6 %collective-permute-start.3 = (bf16[256,2048]{1,0:T(8,128)(2,1)S(1)}, bf16[256,2048]{1,0:T(8,128)(2,1)}, u32[]{:S(2)}, u32[]{:S(2)}) collective-permute-start(bf16[256,2048]{1,0:T(8,128)(2,1)S(1)} %bitcast.193), channel_id=1, source_target_pairs={{0,4},{4,0},{8,12},{12,8},{16,20},{20,16},{24,28},{28,24},{1,5},{5... | collective-permute-start | bytes 3145736 | tf_op jit(solution)/shard_map/ppermute | solution.py:731
  446.9 103.6 %collective-permute-start.4 = (bf16[256,2048]{1,0:T(8,128)(2,1)}, bf16[256,2048]{1,0:T(8,128)(2,1)}, u32[]{:S(2)}, u32[]{:S(2)}) collective-permute-start(bf16[256,2048]{1,0:T(8,128)(2,1)} %collective-permute-done), channel_id=1, source_target_pairs={{0,4},{4,0},{8,12},{12,8},{16,20},{20,16},{24,28},{28,24},{1,5},{5... | collective-permute-start | bytes 3145736 | tf_op jit(solution)/shard_map/ppermute | solution.py:731
  449.0 101.5 %collective-permute-start.5 = (bf16[256,2048]{1,0:T(8,128)(2,1)}, bf16[256,2048]{1,0:T(8,128)(2,1)S(1)}, u32[]{:S(2)}, u32[]{:S(2)}) collective-permute-start(bf16[256,2048]{1,0:T(8,128)(2,1)} %collective-permute-done.1), channel_id=1, source_target_pairs={{0,4},{4,0},{8,12},{12,8},{16,20},{20,16},{24,28},{28,24},{1,5},{5... | collective-permute-start | bytes 3145736 | tf_op jit(solution)/shard_map/ppermute | solution.py:731
  449.0 101.5 %collective-permute-start.6 = (bf16[256,2048]{1,0:T(8,128)(2,1)}, bf16[256,2048]{1,0:T(8,128)(2,1)S(1)}, u32[]{:S(2)}, u32[]{:S(2)}) collective-permute-start(bf16[256,2048]{1,0:T(8,128)(2,1)} %collective-permute-done.2), channel_id=1, source_target_pairs={{0,4},{4,0},{8,12},{12,8},{16,20},{20,16},{24,28},{28,24},{1,5},{5... | collective-permute-start | bytes 3145736 | tf_op jit(solution)/shard_map/ppermute | solution.py:731
  515.6 22.1 %copy-start.40 = (f32[8,4,96]{2,1,0:T(4,128)S(1)}, f32[8,4,96]{2,1,0:T(4,128)}, u32[]{:S(2)}) copy-start(f32[8,4,96]{2,1,0:T(4,128)} %select_reduce_fusion) | copy-start | bytes 36868
  650.9 22.2 %slice-start.4 = ((s8[6291456]{0:T(1024)(128)(4,1)}), s8[4194304]{0:T(1024)(128)(4,1)S(1)}, s32[]{:S(2)}) async-start(s8[6291456]{0:T(1024)(128)(4,1)} %bitcast.214), calls=%async_computation.20 | async-start | bytes 8388608
  650.9 22.2 %slice-start.5 = ((s8[6291456]{0:T(1024)(128)(4,1)}), s8[2097152]{0:T(1024)(128)(4,1)S(1)}, s32[]{:S(2)}) async-start(s8[6291456]{0:T(1024)(128)(4,1)} %bitcast.214), calls=%async_computation.21 | async-start | bytes 4194304
  650.9 89.2 %collective-permute-start.7 = (bf16[4,256,2048]{2,1,0:T(8,128)(2,1)}, bf16[4,256,2048]{2,1,0:T(8,128)(2,1)}, u32[]{:S(2)}, u32[]{:S(2)}) collective-permute-start(bf16[4,256,2048]{2,1,0:T(8,128)(2,1)} %get-tuple-element.121), channel_id=1, source_target_pairs={{0,4},{4,0},{8,12},{12,8},{16,20},{20,16},{24,28},{28,24},{1,5},{5... | collective-permute-start | bytes 12582920 | tf_op jit(solution)/shard_map/ppermute | solution.py:752
  673.1 24.4 %copy-start.33 = (f32[8,4,256]{2,1,0:T(4,128)S(1)}, f32[8,4,256]{2,1,0:T(4,128)}, u32[]{:S(2)}) copy-start(f32[8,4,256]{2,1,0:T(4,128)} %copy-done.32) | copy-start | bytes 98308
  673.1 24.4 %copy-start.35 = (pred[8,4,256]{2,1,0:T(4,128)(4,1)S(1)}, pred[8,4,256]{2,1,0:T(4,128)(4,1)}, u32[]{:S(2)}) copy-start(pred[8,4,256]{2,1,0:T(4,128)(4,1)} %copy-done.34) | copy-start | bytes 24580
  740.1 351.6 %reduce-scatter.8.cloned.1.call-start = ((), (), s32[]{:S(2)}) async-start(), calls=%async_computation.12 | async-start | bytes 20971520 | tf_op jit(solution)/shard_map/reduce_scatter | solution.py:856
  740.7 382.6 %reduce-scatter.10.cloned.1.call-start = ((), (), s32[]{:S(2)}) async-start(), calls=%async_computation.13 | async-start | bytes 20971520 | tf_op jit(solution)/shard_map/reduce_scatter | solution.py:856
  741.5 510.3 %reduce-scatter.12.cloned.1.call-start = ((), (), s32[]{:S(2)}) async-start(), calls=%async_computation.14 | async-start | bytes 3932160 | tf_op jit(solution)/shard_map/reduce_scatter | solution.py:899
  742.8 99.5 %copy-start.24 = (f32[256,2048]{1,0:T(8,128)S(1)}, f32[256,2048]{1,0:T(8,128)}, u32[]{:S(2)}) copy-start(f32[256,2048]{1,0:T(8,128)} %copy-done.23) | copy-start | bytes 6291460
  742.8 99.5 %copy-start.37 = (f32[1,2048]{1,0:T(1,128)S(1)}, f32[1,2048]{1,0:T(1,128)}, u32[]{:S(2)}) copy-start(f32[1,2048]{1,0:T(1,128)} %copy-done.36) | copy-start | bytes 24580
  742.8 99.5 %copy-start.43 = (f32[256]{0:T(256)S(1)}, f32[256]{0:T(256)}, u32[]{:S(2)}) copy-start(f32[256]{0:T(256)} %copy-done.42) | copy-start | bytes 3076
  742.8 102.8 %copy-start.27 = (bf16[1,256,2048]{2,1,0:T(8,128)(2,1)S(1)}, bf16[1,256,2048]{2,1,0:T(8,128)(2,1)}, u32[]{:S(2)}) copy-start(bf16[1,256,2048]{2,1,0:T(8,128)(2,1)} %param.18) | copy-start | bytes 3145732
  960.2 15.1 %slice-start = ((s8[8388608]{0:T(1024)(128)(4,1)}), s8[4194304]{0:T(1024)(128)(4,1)S(1)}, s32[]{:S(2)}) async-start(s8[8388608]{0:T(1024)(128)(4,1)} %bitcast.180), calls=%async_computation.16 | async-start | bytes 8388608
  960.2 15.1 %slice-start.1 = ((s8[8388608]{0:T(1024)(128)(4,1)}), s8[4194304]{0:T(1024)(128)(4,1)S(1)}, s32[]{:S(2)}) async-start(s8[8388608]{0:T(1024)(128)(4,1)} %bitcast.180), calls=%async_computation.17 | async-start | bytes 8388608
  968.2 123.5 %collective-permute-start.10 = (bf16[256,2048]{1,0:T(8,128)(2,1)}, bf16[256,2048]{1,0:T(8,128)(2,1)S(1)}, u32[]{:S(2)}, u32[]{:S(2)}) collective-permute-start(bf16[256,2048]{1,0:T(8,128)(2,1)} %get-tuple-element.123), channel_id=1, source_target_pairs={{0,24},{4,28},{8,0},{12,4},{16,8},{20,12},{24,16},{28,20},{1,25},{... | collective-permute-start | bytes 3145736 | tf_op jit(solution)/shard_map/ppermute | solution.py:762
  974.7 117.0 %collective-permute-start.8 = (bf16[256,2048]{1,0:T(8,128)(2,1)}, bf16[256,2048]{1,0:T(8,128)(2,1)S(1)}, u32[]{:S(2)}, u32[]{:S(2)}) collective-permute-start(bf16[256,2048]{1,0:T(8,128)(2,1)} %get-tuple-element.125), channel_id=1, source_target_pairs={{0,8},{4,12},{8,16},{12,20},{16,24},{20,28},{24,0},{28,4},{1,9},{5... | collective-permute-start | bytes 3145736 | tf_op jit(solution)/shard_map/ppermute | solution.py:762
  974.7 117.0 %collective-permute-start.9 = (bf16[256,2048]{1,0:T(8,128)(2,1)}, bf16[256,2048]{1,0:T(8,128)(2,1)}, u32[]{:S(2)}, u32[]{:S(2)}) collective-permute-start(bf16[256,2048]{1,0:T(8,128)(2,1)} %get-tuple-element.124), channel_id=1, source_target_pairs={{0,16},{4,20},{8,24},{12,28},{16,0},{20,4},{24,8},{28,12},{1,17},{... | collective-permute-start | bytes 3145736 | tf_op jit(solution)/shard_map/ppermute | solution.py:762
  980.0 22.3 %copy-start.4 = (f32[256,128]{1,0:T(8,128)S(1)}, f32[256,128]{1,0:T(8,128)}, u32[]{:S(2)}) copy-start(f32[256,128]{1,0:T(8,128)} %copy-done.3) | copy-start | bytes 393220
  980.0 22.3 %copy-start.6 = (f32[256,128]{1,0:T(8,128)S(1)}, f32[256,128]{1,0:T(8,128)}, u32[]{:S(2)}) copy-start(f32[256,128]{1,0:T(8,128)} %copy-done.5) | copy-start | bytes 393220
  980.0 22.4 %copy-start.8 = (f32[8,128]{1,0:T(8,128)S(1)}, f32[8,128]{1,0:T(8,128)}, u32[]{:S(2)}) copy-start(f32[8,128]{1,0:T(8,128)} %copy-done.7) | copy-start | bytes 12292
  980.0 22.4 %copy-start.10 = (f32[8,128]{1,0:T(8,128)S(1)}, f32[8,128]{1,0:T(8,128)}, u32[]{:S(2)}) copy-start(f32[8,128]{1,0:T(8,128)} %copy-done.9) | copy-start | bytes 12292
  980.0 22.4 %copy-start.12 = (f32[2,256]{1,0:T(2,128)S(1)}, f32[2,256]{1,0:T(2,128)}, u32[]{:S(2)}) copy-start(f32[2,256]{1,0:T(2,128)} %copy-done.11) | copy-start | bytes 6148
  1067.9 9.5 copy-start.22
  1067.9 9.5 copy-start.54
  1067.9 20.4 %slice-start.2 = ((s8[8388608]{0:T(1024)(128)(4,1)}), s8[4194304]{0:T(1024)(128)(4,1)S(1)}, s32[]{:S(2)}) async-start(s8[8388608]{0:T(1024)(128)(4,1)} %bitcast.183), calls=%async_computation.18 | async-start | bytes 8388608
  1077.4 11.0 slice-start.3
  1077.4 11.0 copy-start.28
  1091.7 132.8 %copy-start.30 = (bf16[256,2048]{1,0:T(8,128)(2,1)}, bf16[256,2048]{1,0:T(8,128)(2,1)S(1)}, u32[]{:S(2)}) copy-start(bf16[256,2048]{1,0:T(8,128)(2,1)S(1)} %collective-permute-done.10) | copy-start | bytes 3145732
  1091.7 132.8 %copy-start.31 = (bf16[256,2048]{1,0:T(8,128)(2,1)}, bf16[256,2048]{1,0:T(8,128)(2,1)S(1)}, u32[]{:S(2)}) copy-start(bf16[256,2048]{1,0:T(8,128)(2,1)S(1)} %collective-permute-done.8) | copy-start | bytes 3145732
  1123.4 152.5 %reduce-scatter.14.cloned.1.call-start = ((), (), s32[]{:S(2)}) async-start(), calls=%async_computation.15 | async-start | bytes 1310720 | tf_op jit(solution)/shard_map/reduce_scatter | solution.py:892
  1123.6 101.0 %copy-start.2 = (bf16[1,256,2048]{2,1,0:T(8,128)(2,1)S(1)}, bf16[1,256,2048]{2,1,0:T(8,128)(2,1)}, u32[]{:S(2)}) copy-start(bf16[1,256,2048]{2,1,0:T(8,128)(2,1)} %param.15) | copy-start | bytes 3145732
  1123.6 101.0 %copy-start.39 = (f32[1,2048]{1,0:T(1,128)S(1)}, f32[1,2048]{1,0:T(1,128)}, u32[]{:S(2)}) copy-start(f32[1,2048]{1,0:T(1,128)} %get-tuple-element.132) | copy-start | bytes 24580
  1123.6 101.0 %copy-start.45 = (f32[256]{0:T(256)S(1)}, f32[256]{0:T(256)}, u32[]{:S(2)}) copy-start(f32[256]{0:T(256)} %add_rsqrt_fusion) | copy-start | bytes 3076
  1255.1 14.9 %copy-start.25 = (f32[256,2048]{1,0:T(8,128)S(1)}, f32[256,2048]{1,0:T(8,128)}, u32[]{:S(2)}) copy-start(f32[256,2048]{1,0:T(8,128)} %copy-done.23) | copy-start | bytes 6291460
  1255.1 14.9 %copy-start.38 = (f32[1,2048]{1,0:T(1,128)S(1)}, f32[1,2048]{1,0:T(1,128)}, u32[]{:S(2)}) copy-start(f32[1,2048]{1,0:T(1,128)} %copy-done.36) | copy-start | bytes 24580
  1255.1 14.9 %copy-start.44 = (f32[256]{0:T(256)S(1)}, f32[256]{0:T(256)}, u32[]{:S(2)}) copy-start(f32[256]{0:T(256)} %copy-done.42) | copy-start | bytes 3076
  1255.1 14.9 %copy-start.47 = (f32[256]{0:T(256)S(1)}, f32[256]{0:T(256)}, u32[]{:S(2)}) copy-start(f32[256]{0:T(256)} %copy-done.46) | copy-start | bytes 3076
  1257.6 25.2 %all-to-all-start.1 = ((bf16[8,64,3,256]{3,1,2,0:T(8,128)(2,1)}), bf16[8,64,3,256]{3,1,2,0:T(8,128)(2,1)}, u32[]{:S(2)}, u32[]{:S(2)}) async-start(bf16[8,64,3,256]{3,1,2,0:T(8,128)(2,1)} %copy.116), calls=%async_computation.5 | async-start | bytes 1572864 | tf_op jit(solution)/shard_map/all_to_all | solution.py:901
  (19 other events, 68.5 us)
Sparse Core Ops, SparseCore 0:
  9.6 92.6 all-gather.4
  104.4 104.6 all-gather.6
  211.3 105.8 all-gather.8
  318.6 105.8 all-gather.10
  740.2 127.8 reduce-scatter.5
  870.6 125.0 reduce-scatter.7
  998.3 125.0 reduce-scatter.9
  1125.9 37.8 reduce-scatter.11
  1240.0 24.5 reduce-scatter.13
